TPU v7x, 256 devices: a whole 4x4x8 slice. The times are simulated.
256 devices in a mesh: pb: 16 (over y_hi, x, core), wa: 16 (over y_lo, z).
Axes of the slice: x: 4, y: 4 (y_hi: 2, y_lo: 2; y = y_hi * 2 + y_lo), z: 8, core: 2. Of those that a mesh axis runs over, the one named last changes fastest.
Arguments:
- acts: bfloat16 [4096, 28672], P('pb', 'wa'), may hold values from -6 to 6
- grads: bfloat16 [4096, 8192], P('pb', 'wa'), may hold values from -6 to 6
- query_in: bfloat16 [28672, 4096], P('wa', 'pb'), may hold values from -0.03125 to 0.03125
- query_out: bfloat16 [8192, 4096], P('wa', 'pb'), may hold values from -0.01171875 to 0.01171875
- lengths: int32 [256], replicated, may hold values from 1 to 128, 4096 in all
Outputs:
- seq_scores: float32 [128, 256], P('pb', 'wa')
Inputs may be any that keep to these rules, and one draw needn't show every extreme that they name: The lengths sum to 4096 and the longest is exactly 128.
All inputs are finite; a program needn't handle non-finite values.
Results may differ from a plain program's by a relative error of at most 0.0003.
Values may be sent and summed in bfloat16 or wider, within the bound.
No kernel may reach another device: no remote copies, remote signals or barrier semaphores. Data moves between devices by JAX's collectives and lax.ppermute only.
A program may use at most 64 MiB of HBM per device.

v0:
```python
import jax
import jax.numpy as jnp
from jax import lax
from jax.sharding import PartitionSpec as P


RANK = 32
LANES = 128


def moved(value, pairs):
    return lax.ppermute(value, "pb", pairs)


def project(tokens, queries):
    return jnp.dot(tokens, queries, preferred_element_type=jnp.float32)


def summed(parts, widths):
    both = jnp.concatenate(parts, axis=1)
    rows = both.shape[0] // widths
    came = lax.all_to_all(both, "wa", 0, 0, tiled=True)
    total = jnp.sum(came.reshape(widths, rows, both.shape[1]), axis=0)
    return jnp.split(total, len(parts), axis=1)


def summed_narrow(parts, widths):
    both = jnp.concatenate(parts, axis=1)
    rows, lanes = both.shape[0] // widths, both.shape[1]
    largest = jnp.maximum(jnp.max(jnp.abs(both)), 1e-30)
    power = 13.0 - jnp.ceil(jnp.log2(largest))
    sent = (both * jnp.exp2(power)).astype(jnp.float16)
    tag = jnp.full((both.shape[0], LANES), power, jnp.float16)
    came = lax.all_to_all(jnp.concatenate([sent, tag], axis=1), "wa", 0, 0, tiled=True)
    came = came.reshape(widths, rows, lanes + LANES).astype(jnp.float32)
    undo = jnp.exp2(-came[:, :, lanes : lanes + 1])
    total = jnp.sum(came[:, :, :lanes] * undo, axis=0)
    return jnp.split(total, len(parts), axis=1)


def member_table(starts, ends, first, count):
    spots = first + lax.iota(jnp.int32, count)
    inside = (spots[:, None] >= starts[None, :]) & (spots[:, None] < ends[None, :])
    return inside.astype(jnp.float32)


def scores(acts, grads, query_in, query_out, lengths):
    groups = lax.axis_size("pb")
    widths = lax.axis_size("wa")
    group = lax.axis_index("pb")
    width_slot = lax.axis_index("wa")
    quarter, half = groups // 4, groups // 2
    tok = acts.shape[0]
    rows = tok // widths
    nseq = lengths.shape[0]
    even = group % 2 == 0

    swap = [(p, p ^ 1) for p in range(groups)]
    ahead = [(p, (p + 2) % groups) for p in range(groups)]
    back = [(p, (p - quarter) % groups) for p in range(groups)]
    flip = [(p, (p - 1 + half) % groups) for p in range(1, groups, 2)]

    side_out = moved(grads, swap)
    last_out = moved(grads, ahead)
    far_out = moved(query_out, back)
    flip_out = moved(grads, flip)
    side_in = moved(acts, swap)
    last_in = moved(acts, ahead)
    far_in = moved(query_in, back)
    flip_in = moved(acts, flip)
    lasts_out = moved(last_out, swap)
    lasts_in = moved(last_in, swap)
    edge_out = jnp.where(even, flip_out, side_out)
    edge_in = jnp.where(even, flip_in, side_in)

    own_in = project(acts, query_in)
    own_out = project(grads, query_out)
    rest_out = [
        project(edge_out, query_out),
        project(last_out, query_out),
        project(lasts_out, query_out),
        project(grads, far_out),
        project(side_out, far_out),
        project(last_out, far_out),
        project(lasts_out, far_out),
    ]
    outs = summed([own_out, *rest_out], widths)
    deep_in = [
        project(edge_in, query_in),
        project(last_in, query_in),
        project(lasts_in, query_in),
        project(acts, far_in),
        project(side_in, far_in),
        project(last_in, far_in),
        project(lasts_in, far_in),
    ]
    ins = summed_narrow([own_in, *deep_in], widths)
    ends = jnp.cumsum(lengths)
    starts = ends - lengths

    def table(block):
        return member_table(starts, ends, block * tok + width_slot * rows, rows)

    here, side = group, group ^ 1
    edge = jnp.where(even, (group + groups - half + 1) % groups, side)
    last, lasts = (group + groups - 2) % groups, (side + groups - 2) % groups
    t_own, t_side, t_edge, t_last, t_lasts = [table(b) for b in (here, side, edge, last, lasts)]

    def totals(proj_in, proj_out, tables):
        products = jnp.concatenate([a * b for a, b in zip(proj_in, proj_out)], axis=0)
        table = jnp.concatenate(tables, axis=0)
        by_rank = lax.dot_general(
            products, table, (((0,), (0,)), ((), ())), precision=lax.Precision.HIGHEST
        )
        return jnp.sum(by_rank.reshape(-1, RANK, nseq), axis=1)

    near_total = totals(ins[:4], outs[:4], [t_own, t_edge, t_last, t_lasts])
    far_total = totals(ins[4:], outs[4:], [t_own, t_side, t_last, t_lasts])
    share = nseq // widths
    both = jnp.concatenate([near_total, far_total], axis=0)
    both = jnp.moveaxis(both.reshape(both.shape[0], widths, share), 1, 0)
    came = jnp.sum(lax.all_to_all(both, "wa", 0, 0, tiled=True), axis=0)
    queries = near_total.shape[0]
    forward = [(p, (p + quarter) % groups) for p in range(groups)]
    mine = came[:queries] + moved(came[queries:], forward)
    lengths_float = lengths.astype(jnp.float32)
    my_lengths = lax.dynamic_slice_in_dim(lengths_float, width_slot * share, share, 0)
    return mine / my_lengths[None, :]


def solution(mesh):
    return jax.shard_map(
        scores,
        mesh=mesh,
        in_specs=(P("pb", "wa"), P("pb", "wa"), P("wa", "pb"), P("wa", "pb"), P()),
        out_specs=P("pb", "wa"),
        check_vma=False,
    )
```

profile of v0, /device:TPU:6, one launch (start us, length us, event | category | flops | bytes accessed | tf_op | source)
XLA Modules:
  0.0 180.1 jit_solution(8022260150052593129)
XLA Ops:
  0.0 3.1 %collective-permute-start.2 = (bf16[256,1792]{1,0:T(8,128)(2,1)}, bf16[256,1792]{1,0:T(8,128)(2,1)}, u32[]{:S(2)}, u32[]{:S(2)}) collective-permute-start(bf16[256,1792]{1,0:T(8,128)(2,1)} %param.5), channel_id=1, source_target_pairs={{0,32},{16,48},{32,64},{48,80},{64,96},{80,112},{96,128},{112,144}... | collective-permute-start | bytes 2752520 | tf_op jit(solution)/shard_map/ppermute | solution.py:12
  3.1 1.3 collective-permute-start
  4.4 18.7 %collective-permute-done.2 = bf16[256,1792]{1,0:T(8,128)(2,1)} collective-permute-done((bf16[256,1792]{1,0:T(8,128)(2,1)}, bf16[256,1792]{1,0:T(8,128)(2,1)}, u32[]{:S(2)}, u32[]{:S(2)}) %collective-permute-start.2) | collective-permute-done | bytes 917536 | tf_op jit(solution)/shard_map/ppermute | solution.py:12
  23.1 0.7 collective-permute-start.4
  23.8 1.9 %convolution_dynamic-update-slice_fusion.15 = f32[256,2048]{0,1:T(8,128)S(1)} fusion(bf16[256,1792]{1,0:T(8,128)(2,1)} %param.5, bf16[1792,256]{1,0:T(8,128)(2,1)} %param.7), kind=kOutput, calls=%fused_computation.19 | convolution fusion | flops 234881024 | bytes 2097152 | tf_op jit(solution)/shard_map/dot_general | solution.py:16
  25.8 2.0 %convolution_dynamic-update-slice_fusion.14 = f32[256,2048]{0,1:T(8,128)S(1)} fusion(f32[256,2048]{0,1:T(8,128)S(1)} %convolution_dynamic-update-slice_fusion.15, bf16[1792,256]{1,0:T(8,128)(2,1)} %param.7, bf16[256,1792]{1,0:T(8,128)(2,1)} %collective-permute-done, bf16[256,1792]{1,0:T(8,128)(2,1)} %collective-permute-done.1, pred[]{:T(512)S(6)} %eq.8), kind=kOutput, calls=%fused_computation.18 | convolution fusion | flops 235339776 | bytes 3014657 | tf_op jit(solution)/shard_map/dot_general | solution.py:16
  27.9 1.8 convolution_dynamic-update-slice_fusion.13
  29.6 1.7 convolution_dynamic-update-slice_fusion.12
  31.3 18.6 %collective-permute-done.4 = bf16[1792,256]{1,0:T(8,128)(2,1)S(1)} collective-permute-done((bf16[1792,256]{1,0:T(8,128)(2,1)}, bf16[1792,256]{1,0:T(8,128)(2,1)S(1)}, u32[]{:S(2)}, u32[]{:S(2)}) %collective-permute-start.4) | collective-permute-done | bytes 917536 | tf_op jit(solution)/shard_map/ppermute | solution.py:12
  50.5 1.7 convolution_dynamic-update-slice_fusion.10
  52.1 1.7 convolution_dynamic-update-slice_fusion.9
  53.8 1.7 convolution_dynamic-update-slice_fusion.8
  57.2 1.2 copy.15
  58.4 1.2 concatenate.25.clone
  59.6 8.9 %all-to-all-start = ((f16[16,16,2176]{2,1,0:T(8,128)(2,1)}), f16[16,16,2176]{2,1,0:T(8,128)(2,1)S(1)}, u32[]{:S(2)}, u32[]{:S(2)}) async-start(f16[16,16,2176]{2,1,0:T(8,128)(2,1)} %bitcast), calls=%async_computation | async-start | bytes 2228224 | tf_op jit(solution)/shard_map/all_to_all | solution.py:34
  68.5 4.2 %collective-permute-start.7 = (bf16[256,512]{1,0:T(8,128)(2,1)S(1)}, bf16[256,512]{1,0:T(8,128)(2,1)S(1)}, u32[]{:S(2)}, u32[]{:S(2)}) collective-permute-start(bf16[256,512]{1,0:T(8,128)(2,1)S(1)} %copy-done.3), channel_id=1, source_target_pairs={{0,32},{16,48},{32,64},{48,80},{64,96},{80,112},{96,128},{112,144}... | collective-permute-start | bytes 786440 | tf_op jit(solution)/shard_map/ppermute | solution.py:12
  72.7 1.3 collective-permute-start.5
  74.1 1.0 convolution_dynamic-update-slice_fusion.7
  75.1 8.8 %collective-permute-done.7 = bf16[256,512]{1,0:T(8,128)(2,1)S(1)} collective-permute-done((bf16[256,512]{1,0:T(8,128)(2,1)S(1)}, bf16[256,512]{1,0:T(8,128)(2,1)S(1)}, u32[]{:S(2)}, u32[]{:S(2)}) %collective-permute-start.7) | collective-permute-done | bytes 262176 | tf_op jit(solution)/shard_map/ppermute | solution.py:12
  84.0 10.1 %collective-permute-done.5 = bf16[256,512]{1,0:T(8,128)(2,1)S(1)} collective-permute-done((bf16[256,512]{1,0:T(8,128)(2,1)S(1)}, bf16[256,512]{1,0:T(8,128)(2,1)S(1)}, u32[]{:S(2)}, u32[]{:S(2)}) %collective-permute-start.5) | collective-permute-done | bytes 262176 | tf_op jit(solution)/shard_map/ppermute | solution.py:12
  94.0 1.0 convolution_dynamic-update-slice_fusion.6
  95.0 1.0 convolution_dynamic-update-slice_fusion.5
  96.0 1.0 convolution_dynamic-update-slice_fusion.4
  97.0 1.0 convolution_dynamic-update-slice_fusion.3
  98.0 1.0 convolution_dynamic-update-slice_fusion.2
  99.0 1.0 convolution_dynamic-update-slice_fusion.1
  100.0 1.0 convolution_dynamic-update-slice_fusion
  101.0 2.9 %copy.13 = f32[256,2048]{1,0:T(8,128)} copy(f32[256,2048]{0,1:T(8,128)} %convolution_dynamic-update-slice_fusion) | data formatting | bytes 4194304 | tf_op jit(solution)/shard_map/concatenate | solution.py:20
  103.9 7.8 %all-to-all-start.1 = ((f32[16,16,2048]{2,1,0:T(8,128)}), f32[16,16,2048]{2,1,0:T(8,128)S(1)}, u32[]{:S(2)}, u32[]{:S(2)}) async-start(f32[16,16,2048]{2,1,0:T(8,128)} %bitcast.1), calls=%async_computation.1 | async-start | bytes 4194304 | tf_op jit(solution)/shard_map/all_to_all | solution.py:22
  113.1 45.5 %all-to-all-done.1 = f32[16,16,2048]{2,1,0:T(8,128)S(1)} async-done(((f32[16,16,2048]{2,1,0:T(8,128)}), f32[16,16,2048]{2,1,0:T(8,128)S(1)}, u32[]{:S(2)}, u32[]{:S(2)}) %all-to-all-start.1) | async-done | bytes 2097184 | tf_op jit(solution)/shard_map/all_to_all | solution.py:22
  160.0 13.0 %all_to_all.23 = f32[16,1,256]{2,1,0:T(1,128)S(1)} all-to-all(f32[16,1,256]{2,1,0:T(1,128)S(1)} %reshape.72), channel_id=1, replica_groups=mesh['pb'=16,'wa'=16] {'wa'}, dimensions={0} | all-to-all | bytes 32768 | tf_op jit(solution)/shard_map/all_to_all | solution.py:122
  174.5 5.0 %collective-permute-done.10 = f32[8,16]{1,0:T(8,128)S(1)} collective-permute-done((f32[8,16]{1,0:T(8,128)S(1)}, f32[8,16]{1,0:T(8,128)S(1)}, u32[]{:S(2)}, u32[]{:S(2)}) %collective-permute-start.10) | collective-permute-done | bytes 544 | tf_op jit(solution)/shard_map/ppermute | solution.py:12
  (53 shorter events, 6.2 us)
Async XLA Ops:
  0.0 23.1 %collective-permute-start.2 = (bf16[256,1792]{1,0:T(8,128)(2,1)}, bf16[256,1792]{1,0:T(8,128)(2,1)}, u32[]{:S(2)}, u32[]{:S(2)}) collective-permute-start(bf16[256,1792]{1,0:T(8,128)(2,1)} %param.5), channel_id=1, source_target_pairs={{0,32},{16,48},{32,64},{48,80},{64,96},{80,112},{96,128},{112,144}... | collective-permute-start | bytes 2752520 | tf_op jit(solution)/shard_map/ppermute | solution.py:12
  3.1 22.7 %collective-permute-start.1 = (bf16[256,1792]{1,0:T(8,128)(2,1)}, bf16[256,1792]{1,0:T(8,128)(2,1)}, u32[]{:S(2)}, u32[]{:S(2)}) collective-permute-start(bf16[256,1792]{1,0:T(8,128)(2,1)} %param.5), channel_id=1, source_target_pairs={{0,16},{16,0},{32,48},{48,32},{64,80},{80,64},{96,112},{112,96},{1... | collective-permute-start | bytes 2752520 | tf_op jit(solution)/shard_map/ppermute | solution.py:12
  3.1 22.7 %collective-permute-start = (bf16[256,1792]{1,0:T(8,128)(2,1)}, bf16[256,1792]{1,0:T(8,128)(2,1)}, u32[]{:S(2)}, u32[]{:S(2)}) collective-permute-start(bf16[256,1792]{1,0:T(8,128)(2,1)} %param.5), channel_id=1, source_target_pairs={{16,128},{48,160},{80,192},{112,224},{144,0},{176,32},{208,64},{24... | collective-permute-start | bytes 2752520 | tf_op jit(solution)/shard_map/ppermute | solution.py:12
  23.1 6.6 %collective-permute-start.3 = (bf16[256,1792]{1,0:T(8,128)(2,1)}, bf16[256,1792]{1,0:T(8,128)(2,1)}, u32[]{:S(2)}, u32[]{:S(2)}) collective-permute-start(bf16[256,1792]{1,0:T(8,128)(2,1)} %collective-permute-done.2), channel_id=1, source_target_pairs={{0,16},{16,0},{32,48},{48,32},{64,80},{80,64},{96,112},{112,96},{1... | collective-permute-start | bytes 2752520 | tf_op jit(solution)/shard_map/ppermute | solution.py:12
  23.1 26.9 %collective-permute-start.4 = (bf16[1792,256]{1,0:T(8,128)(2,1)}, bf16[1792,256]{1,0:T(8,128)(2,1)S(1)}, u32[]{:S(2)}, u32[]{:S(2)}) collective-permute-start(bf16[1792,256]{1,0:T(8,128)(2,1)} %param.7), channel_id=1, source_target_pairs={{0,192},{16,208},{32,224},{48,240},{64,0},{80,16},{96,32},{112,48}... | collective-permute-start | bytes 2752520 | tf_op jit(solution)/shard_map/ppermute | solution.py:12
  25.8 2.1 %copy-start = (bf16[1792,256]{1,0:T(8,128)(2,1)S(1)}, bf16[1792,256]{1,0:T(8,128)(2,1)}, u32[]{:S(2)}) copy-start(bf16[1792,256]{1,0:T(8,128)(2,1)} %param.7) | copy-start | bytes 2752516
  27.9 22.1 %copy-start.2 = (bf16[256,1792]{1,0:T(8,128)(2,1)S(1)}, bf16[256,1792]{1,0:T(8,128)(2,1)}, u32[]{:S(2)}) copy-start(bf16[256,1792]{1,0:T(8,128)(2,1)} %param.5) | copy-start | bytes 2752516
  58.4 10.1 %copy-start.3 = (bf16[256,512]{1,0:T(8,128)(2,1)S(1)}, bf16[256,512]{1,0:T(8,128)(2,1)}, u32[]{:S(2)}) copy-start(bf16[256,512]{1,0:T(8,128)(2,1)} %param.6) | copy-start | bytes 786436
  58.4 15.6 %copy-start.1 = (bf16[512,256]{1,0:T(8,128)(2,1)S(1)}, bf16[512,256]{1,0:T(8,128)(2,1)}, u32[]{:S(2)}) copy-start(bf16[512,256]{1,0:T(8,128)(2,1)} %param.8) | copy-start | bytes 786436
  59.6 44.3 %all-to-all-start = ((f16[16,16,2176]{2,1,0:T(8,128)(2,1)}), f16[16,16,2176]{2,1,0:T(8,128)(2,1)S(1)}, u32[]{:S(2)}, u32[]{:S(2)}) async-start(f16[16,16,2176]{2,1,0:T(8,128)(2,1)} %bitcast), calls=%async_computation | async-start | bytes 2228224 | tf_op jit(solution)/shard_map/all_to_all | solution.py:34
  68.5 15.4 %collective-permute-start.7 = (bf16[256,512]{1,0:T(8,128)(2,1)S(1)}, bf16[256,512]{1,0:T(8,128)(2,1)S(1)}, u32[]{:S(2)}, u32[]{:S(2)}) collective-permute-start(bf16[256,512]{1,0:T(8,128)(2,1)S(1)} %copy-done.3), channel_id=1, source_target_pairs={{0,32},{16,48},{32,64},{48,80},{64,96},{80,112},{96,128},{112,144}... | collective-permute-start | bytes 786440 | tf_op jit(solution)/shard_map/ppermute | solution.py:12
  72.7 11.2 %collective-permute-start.6 = (bf16[256,512]{1,0:T(8,128)(2,1)S(1)}, bf16[256,512]{1,0:T(8,128)(2,1)S(1)}, u32[]{:S(2)}, u32[]{:S(2)}) collective-permute-start(bf16[256,512]{1,0:T(8,128)(2,1)S(1)} %copy-done.3), channel_id=1, source_target_pairs={{0,16},{16,0},{32,48},{48,32},{64,80},{80,64},{96,112},{112,96},{1... | collective-permute-start | bytes 786440 | tf_op jit(solution)/shard_map/ppermute | solution.py:12
  72.7 21.3 %collective-permute-start.5 = (bf16[256,512]{1,0:T(8,128)(2,1)S(1)}, bf16[256,512]{1,0:T(8,128)(2,1)S(1)}, u32[]{:S(2)}, u32[]{:S(2)}) collective-permute-start(bf16[256,512]{1,0:T(8,128)(2,1)S(1)} %copy-done.3), channel_id=1, source_target_pairs={{16,128},{48,160},{80,192},{112,224},{144,0},{176,32},{208,64},{24... | collective-permute-start | bytes 786440 | tf_op jit(solution)/shard_map/ppermute | solution.py:12
  74.0 23.0 %collective-permute-start.9 = (bf16[512,256]{1,0:T(8,128)(2,1)S(1)}, bf16[512,256]{1,0:T(8,128)(2,1)S(1)}, u32[]{:S(2)}, u32[]{:S(2)}) collective-permute-start(bf16[512,256]{1,0:T(8,128)(2,1)S(1)} %copy-done.1), channel_id=1, source_target_pairs={{0,192},{16,208},{32,224},{48,240},{64,0},{80,16},{96,32},{112,48}... | collective-permute-start | bytes 786440 | tf_op jit(solution)/shard_map/ppermute | solution.py:12
  84.0 12.0 %collective-permute-start.8 = (bf16[256,512]{1,0:T(8,128)(2,1)S(1)}, bf16[256,512]{1,0:T(8,128)(2,1)S(1)}, u32[]{:S(2)}, u32[]{:S(2)}) collective-permute-start(bf16[256,512]{1,0:T(8,128)(2,1)S(1)} %collective-permute-done.7), channel_id=1, source_target_pairs={{0,16},{16,0},{32,48},{48,32},{64,80},{80,64},{96,112},{112,96},{1... | collective-permute-start | bytes 786440 | tf_op jit(solution)/shard_map/ppermute | solution.py:12
  103.9 7.9 %copy-start.4 = (s32[256]{0:T(256)S(1)}, s32[256]{0:T(256)}, u32[]{:S(2)}) copy-start(s32[256]{0:T(256)} %param.9) | copy-start | bytes 3076
  103.9 54.6 %all-to-all-start.1 = ((f32[16,16,2048]{2,1,0:T(8,128)}), f32[16,16,2048]{2,1,0:T(8,128)S(1)}, u32[]{:S(2)}, u32[]{:S(2)}) async-start(f32[16,16,2048]{2,1,0:T(8,128)} %bitcast.1), calls=%async_computation.1 | async-start | bytes 4194304 | tf_op jit(solution)/shard_map/all_to_all | solution.py:22
  174.3 5.2 %collective-permute-start.10 = (f32[8,16]{1,0:T(8,128)S(1)}, f32[8,16]{1,0:T(8,128)S(1)}, u32[]{:S(2)}, u32[]{:S(2)}) collective-permute-start(f32[8,16]{1,0:T(8,128)S(1)} %slice.28), channel_id=1, source_target_pairs={{0,64},{16,80},{32,96},{48,112},{64,128},{80,144},{96,160},{112,17... | collective-permute-start | bytes 1544 | tf_op jit(solution)/shard_map/ppermute | solution.py:12
where the time goes:
time: 182 us; the launch traced here: 180 us
  waiting for transfers between devices  107 us (59%)
  starting transfers between devices  27.5 us (15%)
  matrix products  21.8 us (12%)
  blocking collectives  13 us (7%)
  local copies, waits for them, and re-layouts  6.44 us (4%)
  other arithmetic  3.41 us (2%)
    ppermute x11, waiting for transfers between devices, moved(): return lax.ppermute(value, 'pb', pairs)  61.2 us
    all_to_all x1, waiting for transfers between devices, summed(): came = lax.all_to_all(both, 'wa', 0, 0, tiled=True)  45.5 us
    dot_general x16, matrix products, project(): return jnp.dot(tokens, queries, preferred_element_type=jnp.float32)  20.8 us
    all_to_all x1, blocking collectives, scores(): came = jnp.sum(lax.all_to_all(both, 'wa', 0, 0, tiled=True), axis=0)  13 us
    ppermute x11, starting transfers between devices, moved(): return lax.ppermute(value, 'pb', pairs)  10.8 us
    all_to_all x1, starting transfers between devices, summed_narrow(): lax.all_to_all(jnp.concatenate([sent, tag], axis=1), 'wa', 0, 0, tiled=True)  8.91 us
    all_to_all x1, starting transfers between devices, summed(): came = lax.all_to_all(both, 'wa', 0, 0, tiled=True)  7.84 us
  transfers between devices with their start and end apart: 13, of which 6 were waited for; matrix products, arithmetic and copies ran while one was open for 11% of the time, Pallas kernels for 0%

commit v1 on v0

v1 whole, which is shorter than its diff:
```python
import functools

import jax
import jax.numpy as jnp
from jax import lax
from jax.experimental import pallas as pl
from jax.experimental.pallas import tpu as pltpu
from jax.sharding import PartitionSpec as P


RANK = 32
LANES = 128


def moved(value, pairs):
    return lax.ppermute(value, "pb", pairs)


def fan_kernel(sides, even_ref, flip_ref, *refs):
    token_refs, query_refs, out_ref = refs[:4], refs[4:-1], refs[-1]
    own_ref, side_ref, last_ref, lasts_ref = token_refs

    def put(slot, tokens, queries):
        width = queries.shape[1]
        out_ref[:, slot * width : (slot + 1) * width] = jnp.dot(
            tokens[...], queries[...], preferred_element_type=jnp.float32
        )

    slot = 0
    for side, queries in zip(sides, query_refs):
        put(slot, own_ref, queries)
        if side == "near":
            at = slot + 1

            @pl.when(even_ref[0] == 1)
            def _():
                put(at, flip_ref, queries)

            @pl.when(even_ref[0] == 0)
            def _():
                put(at, side_ref, queries)

        else:
            put(slot + 1, side_ref, queries)
        put(slot + 2, last_ref, queries)
        put(slot + 3, lasts_ref, queries)
        slot += 4


def fan(sides, even, flip, tokens, queries):
    rows, depth = tokens[0].shape
    width = queries[0].shape[1]
    lanes = 4 * len(sides) * width
    vmem = pl.BlockSpec(memory_space=pltpu.VMEM)
    return pl.pallas_call(
        functools.partial(fan_kernel, sides),
        out_shape=jax.ShapeDtypeStruct((rows, lanes), jnp.float32),
        in_specs=[pl.BlockSpec(memory_space=pltpu.SMEM)] + [vmem] * (5 + len(queries)),
        out_specs=vmem,
        compiler_params=pltpu.CompilerParams(vmem_limit_bytes=16 << 20),
        cost_estimate=pl.CostEstimate(
            flops=2 * rows * depth * lanes,
            bytes_accessed=10 * rows * depth + 2 * depth * width + 4 * rows * lanes,
            transcendentals=0,
        ),
    )(even, flip, *tokens, *queries)


def summed(both, widths):
    rows = both.shape[0] // widths
    came = lax.all_to_all(both, "wa", 0, 0, tiled=True)
    return jnp.sum(came.reshape(widths, rows, both.shape[1]), axis=0)


def summed_narrow(parts, widths):
    rows, lanes = parts[0].shape[0] // widths, sum(p.shape[1] for p in parts)
    largest = functools.reduce(jnp.maximum, [jnp.max(jnp.abs(p)) for p in parts])
    power = 13.0 - jnp.ceil(jnp.log2(jnp.maximum(largest, 1e-30)))
    sent = [(p * jnp.exp2(power)).astype(jnp.float16) for p in parts]
    tag = jnp.full((parts[0].shape[0], LANES), power, jnp.float16)
    came = lax.all_to_all(jnp.concatenate([*sent, tag], axis=1), "wa", 0, 0, tiled=True)
    came = came.reshape(widths, rows, lanes + LANES)
    undo = jnp.exp2(-came[:, :, lanes : lanes + 1].astype(jnp.float32))
    return jnp.sum(came[:, :, :lanes].astype(jnp.float32) * undo, axis=0)


def member_table(starts, ends, first, count):
    spots = first + lax.iota(jnp.int32, count)
    inside = (spots[:, None] >= starts[None, :]) & (spots[:, None] < ends[None, :])
    return inside.astype(jnp.float32)


def scores(acts, grads, query_in, query_out, lengths):
    groups = lax.axis_size("pb")
    widths = lax.axis_size("wa")
    group = lax.axis_index("pb")
    width_slot = lax.axis_index("wa")
    quarter, half = groups // 4, groups // 2
    tok = acts.shape[0]
    rows = tok // widths
    nseq = lengths.shape[0]
    even = group % 2 == 0

    swap = [(p, p ^ 1) for p in range(groups)]
    ahead = [(p, (p + 2) % groups) for p in range(groups)]
    back = [(p, (p - quarter) % groups) for p in range(groups)]
    flip = [(p, (p - 1 + half) % groups) for p in range(1, groups, 2)]

    side_out = moved(grads, swap)
    last_out = moved(grads, ahead)
    far_out = moved(query_out, back)
    flip_out = moved(grads, flip)
    side_in = moved(acts, swap)
    last_in = moved(acts, ahead)
    far_in = moved(query_in, back)
    flip_in = moved(acts, flip)
    lasts_out = moved(last_out, swap)
    lasts_in = moved(last_in, swap)
    parity = even.astype(jnp.int32).reshape(1)
    tokens_out = [grads, side_out, last_out, lasts_out]
    tokens_in = [acts, side_in, last_in, lasts_in]
    both_out = fan(("near", "far"), parity, flip_out, tokens_out, [query_out, far_out])
    outs = summed(both_out, widths)
    near_in = fan(("near",), parity, flip_in, tokens_in, [query_in])
    far_side = fan(("far",), parity, flip_in, tokens_in, [far_in])
    ins = summed_narrow([near_in, far_side], widths)
    products = jnp.split(ins * outs, 8, axis=1)
    ends = jnp.cumsum(lengths)
    starts = ends - lengths

    def table(block):
        return member_table(starts, ends, block * tok + width_slot * rows, rows)

    here, side = group, group ^ 1
    edge = jnp.where(even, (group + groups - half + 1) % groups, side)
    last, lasts = (group + groups - 2) % groups, (side + groups - 2) % groups
    t_own, t_side, t_edge, t_last, t_lasts = [table(b) for b in (here, side, edge, last, lasts)]

    def totals(pieces, tables):
        by_rank = lax.dot_general(
            jnp.concatenate(pieces, axis=0),
            jnp.concatenate(tables, axis=0),
            (((0,), (0,)), ((), ())),
            precision=lax.Precision.HIGHEST,
        )
        return jnp.sum(by_rank.reshape(-1, RANK, nseq), axis=1)

    near_total = totals(products[:4], [t_own, t_edge, t_last, t_lasts])
    far_total = totals(products[4:], [t_own, t_side, t_last, t_lasts])
    share = nseq // widths
    both = jnp.concatenate([near_total, far_total], axis=0)
    both = jnp.moveaxis(both.reshape(both.shape[0], widths, share), 1, 0)
    came = jnp.sum(lax.all_to_all(both, "wa", 0, 0, tiled=True), axis=0)
    queries = near_total.shape[0]
    forward = [(p, (p + quarter) % groups) for p in range(groups)]
    mine = came[:queries] + moved(came[queries:], forward)
    lengths_float = lengths.astype(jnp.float32)
    my_lengths = lax.dynamic_slice_in_dim(lengths_float, width_slot * share, share, 0)
    return mine / my_lengths[None, :]


def solution(mesh):
    return jax.shard_map(
        scores,
        mesh=mesh,
        in_specs=(P("pb", "wa"), P("pb", "wa"), P("wa", "pb"), P("wa", "pb"), P()),
        out_specs=P("pb", "wa"),
        check_vma=False,
    )
```

time: 182 us -> 176 us (0.967)
  the two profiles are of different devices: /device:TPU:6 before, /device:TPU:16 now
where the time goes in v1:
time: 176 us; the launch traced here: 175 us
  waiting for transfers between devices  109 us (62%)
  starting transfers between devices  27.9 us (16%)
  blocking collectives  14.6 us (8%)
  local copies, waits for them, and re-layouts  7.76 us (4%)
  Pallas kernels  7.54 us (4%)
  other arithmetic  5.43 us (3%)
    ppermute x11, waiting for transfers between devices, moved(): return lax.ppermute(value, 'pb', pairs)  57.6 us
    all_to_all x1, waiting for transfers between devices, summed(): came = lax.all_to_all(both, 'wa', 0, 0, tiled=True)  47 us
    all_to_all x1, blocking collectives, scores(): came = jnp.sum(lax.all_to_all(both, 'wa', 0, 0, tiled=True), axis=0)  14.6 us
    ppermute x11, starting transfers between devices, moved(): return lax.ppermute(value, 'pb', pairs)  14 us
    all_to_all x1, starting transfers between devices, summed_narrow(): lax.all_to_all(jnp.concatenate([*sent, tag], axis=1), 'wa', 0, 0, tiled=T...  9.42 us
    pallas_call x3, Pallas kernels, fan(): pl.pallas_call(functools.partial(fan_kernel, sides), out_shape=jax.ShapeD...  7.54 us
    unnamed x24, local copies, waits for them, and re-layouts  6.41 us
    all_to_all x1, waiting for transfers between devices, summed_narrow(): lax.all_to_all(jnp.concatenate([*sent, tag], axis=1), 'wa', 0, 0, tiled=T...  4.66 us
  transfers between devices with their start and end apart: 13, of which 8 were waited for; matrix products, arithmetic and copies ran while one was open for 1% of the time, Pallas kernels for 3%

profile of v1, /device:TPU:16, one launch (start us, length us, event | category | flops | bytes accessed | tf_op | source)
XLA Modules:
  0.0 175.2 jit_solution(15201121625992054541)
XLA Ops:
  0.0 1.5 collective-permute-start.2
  1.5 1.3 collective-permute-start
  2.8 1.4 collective-permute-start.1
  4.2 21.8 %collective-permute-done.2.refs_2_ = bf16[256,1792]{1,0:T(8,128)(2,1)S(1)} collective-permute-done((bf16[256,1792]{1,0:T(8,128)(2,1)}, bf16[256,1792]{1,0:T(8,128)(2,1)S(1)}, u32[]{:S(2)}, u32[]{:S(2)}) %collective-permute-start.2) | collective-permute-done | bytes 917536 | tf_op jit(solution)/shard_map/ppermute | solution.py:16
  26.0 9.7 %collective-permute-done.flip_ref = bf16[256,1792]{1,0:T(8,128)(2,1)S(1)} collective-permute-done((bf16[256,1792]{1,0:T(8,128)(2,1)}, bf16[256,1792]{1,0:T(8,128)(2,1)S(1)}, u32[]{:S(2)}, u32[]{:S(2)}) %collective-permute-start) | collective-permute-done | bytes 917536 | tf_op jit(solution)/shard_map/ppermute | solution.py:16
  35.8 1.0 copy-done.3
  36.7 1.2 copy-done
  37.9 1.2 copy-done.4
  39.1 1.2 copy-done.6
  40.3 2.6 %shard_map.55 = f32[256,1024]{1,0:T(8,128)S(1)} custom-call(s32[1]{0:T(128)} %bitcast.even_ref, bf16[256,1792]{1,0:T(8,128)(2,1)S(1)} %collective-permute-done.flip_ref, bf16[256,1792]{1,0:T(8,128)(2,1)S(1)} %copy-done, bf16[256,1792]{1,0:T(8,128)(2,1)S(1)} %copy-done.4, bf16[256,1792]{1,0:T(8,128)(2,1)S(1)} %collective-permute-done.2.refs_2_, ...), custom_call_target="tpu_custom_call" | custom-call | flops 939524096 | bytes 6553600 | tf_op jit(solution)/shard_map/pallas_call | solution.py:55
  42.9 0.7 abs_reduce_fusion.1
  43.6 7.0 %collective-permute-done.4.refs_4_ = bf16[1792,256]{1,0:T(8,128)(2,1)} collective-permute-done((bf16[1792,256]{1,0:T(8,128)(2,1)}, bf16[1792,256]{1,0:T(8,128)(2,1)}, u32[]{:S(2)}, u32[]{:S(2)}) %collective-permute-start.4) | collective-permute-done | bytes 917536 | tf_op jit(solution)/shard_map/ppermute | solution.py:16
  50.6 1.2 copy-done.2
  51.8 2.6 %shard_map.56 = f32[256,1024]{1,0:T(8,128)S(1)} custom-call(s32[1]{0:T(128)} %bitcast.even_ref, bf16[256,1792]{1,0:T(8,128)(2,1)S(1)} %copy-done.2, bf16[256,1792]{1,0:T(8,128)(2,1)S(1)} %copy-done, bf16[256,1792]{1,0:T(8,128)(2,1)S(1)} %copy-done.5, bf16[256,1792]{1,0:T(8,128)(2,1)S(1)} %collective-permute-done.2.refs_2_, ...), custom_call_target="tpu_custom_call" | custom-call | flops 939524096 | bytes 6553600 | tf_op jit(solution)/shard_map/pallas_call | solution.py:55
  54.3 0.8 abs_reduce_fusion
  56.8 1.3 maximum_maximum_fusion
  58.1 9.4 %all-to-all-start = ((f16[16,16,2176]{2,1,0:T(8,128)(2,1)}), f16[16,16,2176]{2,1,0:T(8,128)(2,1)S(1)}, u32[]{:S(2)}, u32[]{:S(2)}) async-start(f16[16,16,2176]{2,1,0:T(8,128)(2,1)} %bitcast.1), calls=%async_computation | async-start | bytes 2228224 | tf_op jit(solution)/shard_map/all_to_all | solution.py:81
  67.6 1.3 collective-permute-start.5
  68.9 1.5 collective-permute-start.6
  70.4 5.2 %collective-permute-start.9 = (bf16[512,256]{1,0:T(8,128)(2,1)S(1)}, bf16[512,256]{1,0:T(8,128)(2,1)S(1)}, u32[]{:S(2)}, u32[]{:S(2)}) collective-permute-start(bf16[512,256]{1,0:T(8,128)(2,1)S(1)} %copy-done.8), channel_id=1, source_target_pairs={{0,192},{16,208},{32,224},{48,240},{64,0},{80,16},{96,32},{112,48}... | collective-permute-start | bytes 786440 | tf_op jit(solution)/shard_map/ppermute | solution.py:16
  75.6 10.9 %collective-permute-done.7.refs_2_ = bf16[256,512]{1,0:T(8,128)(2,1)S(1)} collective-permute-done((bf16[256,512]{1,0:T(8,128)(2,1)S(1)}, bf16[256,512]{1,0:T(8,128)(2,1)S(1)}, u32[]{:S(2)}, u32[]{:S(2)}) %collective-permute-start.7) | collective-permute-done | bytes 262176 | tf_op jit(solution)/shard_map/ppermute | solution.py:16
  86.5 2.3 %collective-permute-done.5.flip_ref = bf16[256,512]{1,0:T(8,128)(2,1)S(1)} collective-permute-done((bf16[256,512]{1,0:T(8,128)(2,1)S(1)}, bf16[256,512]{1,0:T(8,128)(2,1)S(1)}, u32[]{:S(2)}, u32[]{:S(2)}) %collective-permute-start.5) | collective-permute-done | bytes 262176 | tf_op jit(solution)/shard_map/ppermute | solution.py:16
  88.9 2.4 %shard_map.57 = f32[256,2048]{1,0:T(8,128)} custom-call(s32[1]{0:T(128)} %bitcast.even_ref, bf16[256,512]{1,0:T(8,128)(2,1)S(1)} %collective-permute-done.5.flip_ref, bf16[256,512]{1,0:T(8,128)(2,1)S(1)} %copy-done.7, bf16[256,512]{1,0:T(8,128)(2,1)S(1)} %collective-permute-done.6.refs_1_, bf16[256,512]{1,0:T(8,128)(2,1)S(1)} %collective-permute-done.7.refs_2_, ...), custom_call_target="tpu_custom_call" | custom-call | flops 536870912 | bytes 3670016 | tf_op jit(solution)/shard_map/pallas_call | solution.py:55
  91.2 4.7 %all-to-all-done = f16[16,16,2176]{2,1,0:T(8,128)(2,1)S(1)} async-done(((f16[16,16,2176]{2,1,0:T(8,128)(2,1)}), f16[16,16,2176]{2,1,0:T(8,128)(2,1)S(1)}, u32[]{:S(2)}, u32[]{:S(2)}) %all-to-all-start) | async-done | bytes 1114144 | tf_op jit(solution)/shard_map/all_to_all | solution.py:81
  95.9 4.5 %all-to-all-start.1 = ((f32[16,16,2048]{2,1,0:T(8,128)}), f32[16,16,2048]{2,1,0:T(8,128)S(1)}, u32[]{:S(2)}, u32[]{:S(2)}) async-start(f32[16,16,2048]{2,1,0:T(8,128)} %bitcast.3), calls=%async_computation.1 | async-start | bytes 4194304 | tf_op jit(solution)/shard_map/all_to_all | solution.py:71
  102.1 47.0 %all-to-all-done.1 = f32[16,16,2048]{2,1,0:T(8,128)S(1)} async-done(((f32[16,16,2048]{2,1,0:T(8,128)}), f32[16,16,2048]{2,1,0:T(8,128)S(1)}, u32[]{:S(2)}, u32[]{:S(2)}) %all-to-all-start.1) | async-done | bytes 2097184 | tf_op jit(solution)/shard_map/all_to_all | solution.py:71
  149.7 0.5 bitcast_reduce_fusion
  151.1 14.6 %all_to_all.23 = f32[16,1,256]{2,1,0:T(1,128)S(1)} all-to-all(f32[16,1,256]{2,1,0:T(1,128)S(1)} %reshape.80), channel_id=1, replica_groups=mesh['pb'=16,'wa'=16] {'wa'}, dimensions={0} | all-to-all | bytes 32768 | tf_op jit(solution)/shard_map/all_to_all | solution.py:153
  166.2 0.7 reduce.3
  167.0 1.7 collective-permute-start.10
  168.8 5.8 %collective-permute-done.10 = f32[8,16]{1,0:T(8,128)S(1)} collective-permute-done((f32[8,16]{1,0:T(8,128)S(1)}, f32[8,16]{1,0:T(8,128)S(1)}, u32[]{:S(2)}, u32[]{:S(2)}) %collective-permute-start.10) | collective-permute-done | bytes 544 | tf_op jit(solution)/shard_map/ppermute | solution.py:16
  174.6 0.6 fusion.22
  (55 shorter events, 4.1 us)
Async XLA Ops:
  0.0 26.0 %collective-permute-start.2 = (bf16[256,1792]{1,0:T(8,128)(2,1)}, bf16[256,1792]{1,0:T(8,128)(2,1)S(1)}, u32[]{:S(2)}, u32[]{:S(2)}) collective-permute-start(bf16[256,1792]{1,0:T(8,128)(2,1)} %refs_0_.4), channel_id=1, source_target_pairs={{0,32},{16,48},{32,64},{48,80},{64,96},{80,112},{96,128},{112,144}... | collective-permute-start | bytes 2752520 | tf_op jit(solution)/shard_map/ppermute | solution.py:16
  1.5 34.3 %collective-permute-start = (bf16[256,1792]{1,0:T(8,128)(2,1)}, bf16[256,1792]{1,0:T(8,128)(2,1)S(1)}, u32[]{:S(2)}, u32[]{:S(2)}) collective-permute-start(bf16[256,1792]{1,0:T(8,128)(2,1)} %refs_0_.4), channel_id=1, source_target_pairs={{16,128},{48,160},{80,192},{112,224},{144,0},{176,32},{208,64},{24... | collective-permute-start | bytes 2752520 | tf_op jit(solution)/shard_map/ppermute | solution.py:16
  2.8 33.0 %collective-permute-start.1 = (bf16[256,1792]{1,0:T(8,128)(2,1)}, bf16[256,1792]{1,0:T(8,128)(2,1)S(1)}, u32[]{:S(2)}, u32[]{:S(2)}) collective-permute-start(bf16[256,1792]{1,0:T(8,128)(2,1)} %refs_0_.4), channel_id=1, source_target_pairs={{0,16},{16,0},{32,48},{48,32},{64,80},{80,64},{96,112},{112,96},{1... | collective-permute-start | bytes 2752520 | tf_op jit(solution)/shard_map/ppermute | solution.py:16
  26.0 10.7 %collective-permute-start.3 = (bf16[256,1792]{1,0:T(8,128)(2,1)S(1)}, bf16[256,1792]{1,0:T(8,128)(2,1)}, u32[]{:S(2)}, u32[]{:S(2)}) collective-permute-start(bf16[256,1792]{1,0:T(8,128)(2,1)S(1)} %collective-permute-done.2.refs_2_), channel_id=1, source_target_pairs={{0,16},{16,0},{32,48},{48,32},{64,80},{80,64},{96,112},{112,96},{1... | collective-permute-start | bytes 2752520 | tf_op jit(solution)/shard_map/ppermute | solution.py:16
  26.0 24.6 %collective-permute-start.4 = (bf16[1792,256]{1,0:T(8,128)(2,1)}, bf16[1792,256]{1,0:T(8,128)(2,1)}, u32[]{:S(2)}, u32[]{:S(2)}) collective-permute-start(bf16[1792,256]{1,0:T(8,128)(2,1)} %refs_4_.2), channel_id=1, source_target_pairs={{0,192},{16,208},{32,224},{48,240},{64,0},{80,16},{96,32},{112,48}... | collective-permute-start | bytes 2752520 | tf_op jit(solution)/shard_map/ppermute | solution.py:16
  35.7 7.1 %copy-start.1 = (bf16[256,1792]{1,0:T(8,128)(2,1)}, bf16[256,1792]{1,0:T(8,128)(2,1)S(1)}, u32[]{:S(2)}) copy-start(bf16[256,1792]{1,0:T(8,128)(2,1)S(1)} %collective-permute-done.flip_ref) | copy-start | bytes 2752516
  35.8 1.0 copy-start.3
  36.7 1.2 copy-start
  37.9 1.2 copy-start.4
  39.1 1.2 copy-start.6
  42.9 7.7 %copy-start.5 = (bf16[256,1792]{1,0:T(8,128)(2,1)S(1)}, bf16[256,1792]{1,0:T(8,128)(2,1)}, u32[]{:S(2)}) copy-start(bf16[256,1792]{1,0:T(8,128)(2,1)} %copy-done.3) | copy-start | bytes 2752516
  50.6 1.2 copy-start.2
  58.1 9.4 %copy-start.7 = (bf16[256,512]{1,0:T(8,128)(2,1)S(1)}, bf16[256,512]{1,0:T(8,128)(2,1)}, u32[]{:S(2)}) copy-start(bf16[256,512]{1,0:T(8,128)(2,1)} %refs_0_.5) | copy-start | bytes 786436
  58.1 12.3 %copy-start.8 = (bf16[512,256]{1,0:T(8,128)(2,1)S(1)}, bf16[512,256]{1,0:T(8,128)(2,1)}, u32[]{:S(2)}) copy-start(bf16[512,256]{1,0:T(8,128)(2,1)} %refs_4_.3) | copy-start | bytes 786436
  58.1 37.8 %all-to-all-start = ((f16[16,16,2176]{2,1,0:T(8,128)(2,1)}), f16[16,16,2176]{2,1,0:T(8,128)(2,1)S(1)}, u32[]{:S(2)}, u32[]{:S(2)}) async-start(f16[16,16,2176]{2,1,0:T(8,128)(2,1)} %bitcast.1), calls=%async_computation | async-start | bytes 2228224 | tf_op jit(solution)/shard_map/all_to_all | solution.py:81
  67.5 19.0 %collective-permute-start.7 = (bf16[256,512]{1,0:T(8,128)(2,1)S(1)}, bf16[256,512]{1,0:T(8,128)(2,1)S(1)}, u32[]{:S(2)}, u32[]{:S(2)}) collective-permute-start(bf16[256,512]{1,0:T(8,128)(2,1)S(1)} %copy-done.7), channel_id=1, source_target_pairs={{0,32},{16,48},{32,64},{48,80},{64,96},{80,112},{96,128},{112,144}... | collective-permute-start | bytes 786440 | tf_op jit(solution)/shard_map/ppermute | solution.py:16
  67.6 21.2 %collective-permute-start.5 = (bf16[256,512]{1,0:T(8,128)(2,1)S(1)}, bf16[256,512]{1,0:T(8,128)(2,1)S(1)}, u32[]{:S(2)}, u32[]{:S(2)}) collective-permute-start(bf16[256,512]{1,0:T(8,128)(2,1)S(1)} %copy-done.7), channel_id=1, source_target_pairs={{16,128},{48,160},{80,192},{112,224},{144,0},{176,32},{208,64},{24... | collective-permute-start | bytes 786440 | tf_op jit(solution)/shard_map/ppermute | solution.py:16
  68.9 19.9 %collective-permute-start.6 = (bf16[256,512]{1,0:T(8,128)(2,1)S(1)}, bf16[256,512]{1,0:T(8,128)(2,1)S(1)}, u32[]{:S(2)}, u32[]{:S(2)}) collective-permute-start(bf16[256,512]{1,0:T(8,128)(2,1)S(1)} %copy-done.7), channel_id=1, source_target_pairs={{0,16},{16,0},{32,48},{48,32},{64,80},{80,64},{96,112},{112,96},{1... | collective-permute-start | bytes 786440 | tf_op jit(solution)/shard_map/ppermute | solution.py:16
  70.4 18.5 %collective-permute-start.9 = (bf16[512,256]{1,0:T(8,128)(2,1)S(1)}, bf16[512,256]{1,0:T(8,128)(2,1)S(1)}, u32[]{:S(2)}, u32[]{:S(2)}) collective-permute-start(bf16[512,256]{1,0:T(8,128)(2,1)S(1)} %copy-done.8), channel_id=1, source_target_pairs={{0,192},{16,208},{32,224},{48,240},{64,0},{80,16},{96,32},{112,48}... | collective-permute-start | bytes 786440 | tf_op jit(solution)/shard_map/ppermute | solution.py:16
  86.5 2.4 %collective-permute-start.8 = (bf16[256,512]{1,0:T(8,128)(2,1)S(1)}, bf16[256,512]{1,0:T(8,128)(2,1)S(1)}, u32[]{:S(2)}, u32[]{:S(2)}) collective-permute-start(bf16[256,512]{1,0:T(8,128)(2,1)S(1)} %collective-permute-done.7.refs_2_), channel_id=1, source_target_pairs={{0,16},{16,0},{32,48},{48,32},{64,80},{80,64},{96,112},{112,96},{1... | collective-permute-start | bytes 786440 | tf_op jit(solution)/shard_map/ppermute | solution.py:16
  95.9 4.5 %copy-start.9 = (s32[256]{0:T(256)S(1)}, s32[256]{0:T(256)}, u32[]{:S(2)}) copy-start(s32[256]{0:T(256)} %param.9) | copy-start | bytes 3076
  95.9 53.2 %all-to-all-start.1 = ((f32[16,16,2048]{2,1,0:T(8,128)}), f32[16,16,2048]{2,1,0:T(8,128)S(1)}, u32[]{:S(2)}, u32[]{:S(2)}) async-start(f32[16,16,2048]{2,1,0:T(8,128)} %bitcast.3), calls=%async_computation.1 | async-start | bytes 4194304 | tf_op jit(solution)/shard_map/all_to_all | solution.py:71
  167.0 7.6 %collective-permute-start.10 = (f32[8,16]{1,0:T(8,128)S(1)}, f32[8,16]{1,0:T(8,128)S(1)}, u32[]{:S(2)}, u32[]{:S(2)}) collective-permute-start(f32[8,16]{1,0:T(8,128)S(1)} %slice.28), channel_id=1, source_target_pairs={{0,64},{16,80},{32,96},{48,112},{64,128},{80,144},{96,160},{112,17... | collective-permute-start | bytes 1544 | tf_op jit(solution)/shard_map/ppermute | solution.py:16

commit v2 on v1

--- a/solution.py
+++ b/solution.py
@@ -10,6 +10,8 @@
 
 RANK = 32
 LANES = 128
+LARGEST = 32000.0
+WIDTH = 256
 
 
 def moved(value, pairs):
@@ -20,11 +22,21 @@
     token_refs, query_refs, out_ref = refs[:4], refs[4:-1], refs[-1]
     own_ref, side_ref, last_ref, lasts_ref = token_refs
 
+    rows, tags = out_ref.shape[0], out_ref.shape[1] - LANES
+    lane = lax.broadcasted_iota(jnp.int32, (rows, LANES), 1)
+
     def put(slot, tokens, queries):
         width = queries.shape[1]
-        out_ref[:, slot * width : (slot + 1) * width] = jnp.dot(
-            tokens[...], queries[...], preferred_element_type=jnp.float32
-        )
+        part = jnp.dot(tokens[...], queries[...], preferred_element_type=jnp.float32)
+        largest = jnp.maximum(jnp.max(jnp.abs(part), axis=1, keepdims=True), 1e-25)
+        power = jnp.floor(jnp.log2(LARGEST / largest))
+        coded = jnp.round(part * jnp.exp2(power)).astype(jnp.int32)
+        out_ref[:, slot * width : (slot + 1) * width] = coded.astype(jnp.int16)
+        held = out_ref[:, tags:].astype(jnp.int32)
+        tag = jnp.where(lane == slot, power.astype(jnp.int32), held)
+        out_ref[:, tags:] = tag.astype(jnp.int16)
+
+    out_ref[:, tags:] = jnp.zeros((rows, LANES), jnp.int16)
 
     slot = 0
     for side, queries in zip(sides, query_refs):
@@ -54,34 +66,35 @@
     vmem = pl.BlockSpec(memory_space=pltpu.VMEM)
     return pl.pallas_call(
         functools.partial(fan_kernel, sides),
-        out_shape=jax.ShapeDtypeStruct((rows, lanes), jnp.float32),
+        out_shape=jax.ShapeDtypeStruct((rows, lanes + LANES), jnp.int16),
         in_specs=[pl.BlockSpec(memory_space=pltpu.SMEM)] + [vmem] * (5 + len(queries)),
         out_specs=vmem,
         compiler_params=pltpu.CompilerParams(vmem_limit_bytes=16 << 20),
         cost_estimate=pl.CostEstimate(
             flops=2 * rows * depth * lanes,
-            bytes_accessed=10 * rows * depth + 2 * depth * width + 4 * rows * lanes,
+            bytes_accessed=10 * rows * depth + 2 * depth * width + 2 * rows * lanes,
             transcendentals=0,
         ),
     )(even, flip, *tokens, *queries)
 
 
-def summed(both, widths):
-    rows = both.shape[0] // widths
+def summed(coded, widths):
+    rows = coded[0].shape[0] // widths
+    both = jnp.concatenate(coded, axis=1) if len(coded) > 1 else coded[0]
     came = lax.all_to_all(both, "wa", 0, 0, tiled=True)
-    return jnp.sum(came.reshape(widths, rows, both.shape[1]), axis=0)
-
-
-def summed_narrow(parts, widths):
-    rows, lanes = parts[0].shape[0] // widths, sum(p.shape[1] for p in parts)
-    largest = functools.reduce(jnp.maximum, [jnp.max(jnp.abs(p)) for p in parts])
-    power = 13.0 - jnp.ceil(jnp.log2(jnp.maximum(largest, 1e-30)))
-    sent = [(p * jnp.exp2(power)).astype(jnp.float16) for p in parts]
-    tag = jnp.full((parts[0].shape[0], LANES), power, jnp.float16)
-    came = lax.all_to_all(jnp.concatenate([*sent, tag], axis=1), "wa", 0, 0, tiled=True)
-    came = came.reshape(widths, rows, lanes + LANES)
-    undo = jnp.exp2(-came[:, :, lanes : lanes + 1].astype(jnp.float32))
-    return jnp.sum(came[:, :, :lanes].astype(jnp.float32) * undo, axis=0)
+    came = came.reshape(widths, rows, both.shape[1])
+    pieces, at = [], 0
+    for part in coded:
+        tags = part.shape[1] - LANES
+        slots = tags // WIDTH
+        powers = came[:, :, at + tags : at + tags + slots].astype(jnp.float32)
+        undo = jnp.exp2(-powers)
+        for slot in range(slots):
+            values = came[:, :, at + slot * WIDTH : at + (slot + 1) * WIDTH]
+            scale = undo[:, :, slot : slot + 1]
+            pieces.append(jnp.sum(values.astype(jnp.float32) * scale, axis=0))
+        at += part.shape[1]
+    return pieces
 
 
 def member_table(starts, ends, first, count):
@@ -120,11 +133,11 @@
     tokens_out = [grads, side_out, last_out, lasts_out]
     tokens_in = [acts, side_in, last_in, lasts_in]
     both_out = fan(("near", "far"), parity, flip_out, tokens_out, [query_out, far_out])
-    outs = summed(both_out, widths)
+    outs = summed([both_out], widths)
     near_in = fan(("near",), parity, flip_in, tokens_in, [query_in])
     far_side = fan(("far",), parity, flip_in, tokens_in, [far_in])
-    ins = summed_narrow([near_in, far_side], widths)
-    products = jnp.split(ins * outs, 8, axis=1)
+    ins = summed([near_in, far_side], widths)
+    products = [a * b for a, b in zip(ins, outs)]
     ends = jnp.cumsum(lengths)
     starts = ends - lengths
 

time: 176 us -> 163 us (0.926)
  the two profiles are of different devices: /device:TPU:16 before, /device:TPU:6 now
where the time goes in v2:
time: 163 us
  waiting for transfers between devices  90.7 us (56%)
  starting transfers between devices  40.9 us (25%)
  blocking collectives  13 us (8%)
  local copies, waits for them, and re-layouts  5.98 us (4%)
  Pallas kernels  5.62 us (3%)
  other arithmetic  5.34 us (3%)
    ppermute x11, waiting for transfers between devices, moved(): return lax.ppermute(value, 'pb', pairs)  66.1 us
    all_to_all x2, waiting for transfers between devices, summed(): came = lax.all_to_all(both, 'wa', 0, 0, tiled=True)  24.7 us
    all_to_all x2, starting transfers between devices, summed(): came = lax.all_to_all(both, 'wa', 0, 0, tiled=True)  23.3 us
    ppermute x11, starting transfers between devices, moved(): return lax.ppermute(value, 'pb', pairs)  17.6 us
    all_to_all x1, blocking collectives, scores(): came = jnp.sum(lax.all_to_all(both, 'wa', 0, 0, tiled=True), axis=0)  13 us
    pallas_call x3, Pallas kernels, fan(): pl.pallas_call(functools.partial(fan_kernel, sides), out_shape=jax.ShapeD...  5.62 us
    unnamed x31, local copies, waits for them, and re-layouts  4.18 us
  transfers between devices with their start and end apart: 13, of which 6 were waited for; matrix products, arithmetic and copies ran while one was open for 3% of the time, Pallas kernels for 3%

profile of v2, /device:TPU:6, one launch (start us, length us, event | category | flops | bytes accessed | tf_op | source)
XLA Modules:
  0.0 163.0 jit_solution(180090396217937718)
XLA Ops:
  0.0 3.1 %collective-permute-start.7 = (bf16[256,512]{1,0:T(8,128)(2,1)}, bf16[256,512]{1,0:T(8,128)(2,1)S(1)}, u32[]{:S(2)}, u32[]{:S(2)}) collective-permute-start(bf16[256,512]{1,0:T(8,128)(2,1)} %refs_0_.5), channel_id=1, source_target_pairs={{0,32},{16,48},{32,64},{48,80},{64,96},{80,112},{96,128},{112,144}... | collective-permute-start | bytes 786440 | tf_op jit(solution)/shard_map/ppermute | solution.py:18
  3.1 1.3 collective-permute-start.5
  4.4 2.9 %collective-permute-start.6 = (bf16[256,512]{1,0:T(8,128)(2,1)}, bf16[256,512]{1,0:T(8,128)(2,1)S(1)}, u32[]{:S(2)}, u32[]{:S(2)}) collective-permute-start(bf16[256,512]{1,0:T(8,128)(2,1)} %refs_0_.5), channel_id=1, source_target_pairs={{0,16},{16,0},{32,48},{48,32},{64,80},{80,64},{96,112},{112,96},{1... | collective-permute-start | bytes 786440 | tf_op jit(solution)/shard_map/ppermute | solution.py:18
  7.3 0.9 collective-permute-start.9
  8.2 6.5 %collective-permute-done.7.refs_2_ = bf16[256,512]{1,0:T(8,128)(2,1)S(1)} collective-permute-done((bf16[256,512]{1,0:T(8,128)(2,1)}, bf16[256,512]{1,0:T(8,128)(2,1)S(1)}, u32[]{:S(2)}, u32[]{:S(2)}) %collective-permute-start.7) | collective-permute-done | bytes 262176 | tf_op jit(solution)/shard_map/ppermute | solution.py:18
  14.7 6.0 %collective-permute-start.2 = (bf16[256,1792]{1,0:T(8,128)(2,1)}, bf16[256,1792]{1,0:T(8,128)(2,1)S(1)}, u32[]{:S(2)}, u32[]{:S(2)}) collective-permute-start(bf16[256,1792]{1,0:T(8,128)(2,1)} %refs_0_.4), channel_id=1, source_target_pairs={{0,32},{16,48},{32,64},{48,80},{64,96},{80,112},{96,128},{112,144}... | collective-permute-start | bytes 2752520 | tf_op jit(solution)/shard_map/ppermute | solution.py:18
  20.7 0.9 copy-done.2
  21.6 0.9 copy-done.3
  22.5 2.5 %shard_map.57 = s16[256,2176]{1,0:T(8,128)(2,1)} custom-call(s32[1]{0:T(128)} %bitcast.even_ref, bf16[256,512]{1,0:T(8,128)(2,1)S(1)} %collective-permute-done.5.flip_ref, bf16[256,512]{1,0:T(8,128)(2,1)S(1)} %copy-done.2, bf16[256,512]{1,0:T(8,128)(2,1)S(1)} %collective-permute-done.6.refs_1_, bf16[256,512]{1,0:T(8,128)(2,1)S(1)} %collective-permute-done.7.refs_2_, ...), custom_call_target="tpu_custom_call" | custom-call | flops 536870912 | bytes 2621440 | tf_op jit(solution)/shard_map/pallas_call | solution.py:67
  25.0 8.9 %all-to-all-start.1 = ((s16[16,16,2176]{2,1,0:T(8,128)(2,1)}), s16[16,16,2176]{2,1,0:T(8,128)(2,1)}, u32[]{:S(2)}, u32[]{:S(2)}) async-start(s16[16,16,2176]{2,1,0:T(8,128)(2,1)} %bitcast.3), calls=%async_computation.1 | async-start | bytes 2228224 | tf_op jit(solution)/shard_map/all_to_all | solution.py:84
  33.9 1.3 collective-permute-start
  35.2 2.0 %collective-permute-start.1 = (bf16[256,1792]{1,0:T(8,128)(2,1)S(1)}, bf16[256,1792]{1,0:T(8,128)(2,1)S(1)}, u32[]{:S(2)}, u32[]{:S(2)}) collective-permute-start(bf16[256,1792]{1,0:T(8,128)(2,1)S(1)} %copy-done), channel_id=1, source_target_pairs={{0,16},{16,0},{32,48},{48,32},{64,80},{80,64},{96,112},{112,96},{1... | collective-permute-start | bytes 2752520 | tf_op jit(solution)/shard_map/ppermute | solution.py:18
  37.2 27.1 %collective-permute-done.2.refs_2_ = bf16[256,1792]{1,0:T(8,128)(2,1)S(1)} collective-permute-done((bf16[256,1792]{1,0:T(8,128)(2,1)}, bf16[256,1792]{1,0:T(8,128)(2,1)S(1)}, u32[]{:S(2)}, u32[]{:S(2)}) %collective-permute-start.2) | collective-permute-done | bytes 917536 | tf_op jit(solution)/shard_map/ppermute | solution.py:18
  64.4 2.4 %collective-permute-done.3.refs_3_ = bf16[256,1792]{1,0:T(8,128)(2,1)S(1)} collective-permute-done((bf16[256,1792]{1,0:T(8,128)(2,1)S(1)}, bf16[256,1792]{1,0:T(8,128)(2,1)S(1)}, u32[]{:S(2)}, u32[]{:S(2)}) %collective-permute-start.3) | collective-permute-done | bytes 917536 | tf_op jit(solution)/shard_map/ppermute | solution.py:18
  66.8 1.8 %shard_map.55 = s16[256,1152]{1,0:T(8,128)(2,1)S(1)} custom-call(s32[1]{0:T(128)} %bitcast.even_ref, bf16[256,1792]{1,0:T(8,128)(2,1)S(1)} %collective-permute-done.flip_ref, bf16[256,1792]{1,0:T(8,128)(2,1)S(1)} %copy-done, bf16[256,1792]{1,0:T(8,128)(2,1)S(1)} %collective-permute-done.1.refs_1_, bf16[256,1792]{1,0:T(8,128)(2,1)S(1)} %collective-permute-done.2.refs_2_, ...), custom_call_target="tpu_custom_call" | custom-call | flops 939524096 | bytes 6029312 | tf_op jit(solution)/shard_map/pallas_call | solution.py:67
  68.7 25.0 %collective-permute-done.4.refs_4_ = bf16[1792,256]{1,0:T(8,128)(2,1)S(1)} collective-permute-done((bf16[1792,256]{1,0:T(8,128)(2,1)S(1)}, bf16[1792,256]{1,0:T(8,128)(2,1)S(1)}, u32[]{:S(2)}, u32[]{:S(2)}) %collective-permute-start.4) | collective-permute-done | bytes 917536 | tf_op jit(solution)/shard_map/ppermute | solution.py:18
  93.7 1.3 shard_map.56
  95.0 1.1 pad_add_fusion
  96.1 14.4 %all-to-all-start = ((s16[16,16,2304]{2,1,0:T(8,128)(2,1)}), s16[16,16,2304]{2,1,0:T(8,128)(2,1)S(1)}, u32[]{:S(2)}, u32[]{:S(2)}) async-start(s16[16,16,2304]{2,1,0:T(8,128)(2,1)} %bitcast.1), calls=%async_computation | async-start | bytes 2359296 | tf_op jit(solution)/shard_map/all_to_all | solution.py:84
  110.6 0.3 reduce-window.9
  111.4 0.8 slice.161
  112.4 1.8 %multiply_reduce_fusion.14 = (f32[16,256]{1,0:T(8,128)S(1)}, f32[16,256]{1,0:T(8,128)S(1)}, f32[16,256]{1,0:T(8,128)S(1)}, f32[16,256]{1,0:T(8,128)S(1)}, f32[16...) fusion(s16[16,16,2176]{2,1,0:T(8,128)(2,1)} %all-to-all-done.1, ...), kind=kLoop, calls=%fused_computation.17 | loop fusion | flops 1540096 | bytes 1187840 | tf_op jit(solution)/shard_map/reduce_sum | solution.py:95
  114.9 24.7 %all-to-all-done = s16[16,16,2304]{2,1,0:T(8,128)(2,1)S(1)} async-done(((s16[16,16,2304]{2,1,0:T(8,128)(2,1)}), s16[16,16,2304]{2,1,0:T(8,128)(2,1)S(1)}, u32[]{:S(2)}, u32[]{:S(2)}) %all-to-all-start) | async-done | bytes 1179680 | tf_op jit(solution)/shard_map/all_to_all | solution.py:84
  139.6 0.2 copy.65
  140.1 0.4 multiply_reduce_fusion.15
  141.5 0.5 bitcast_reduce_fusion
  142.1 0.5 bitcast_reduce_fusion.1
  142.9 13.0 %all_to_all.23 = f32[16,1,256]{2,1,0:T(1,128)S(1)} all-to-all(f32[16,1,256]{2,1,0:T(1,128)S(1)} %reshape.80), channel_id=1, replica_groups=mesh['pb'=16,'wa'=16] {'wa'}, dimensions={0} | all-to-all | bytes 32768 | tf_op jit(solution)/shard_map/all_to_all | solution.py:166
  155.9 0.5 broadcast.42
  156.4 0.7 reduce.2
  157.4 5.0 %collective-permute-done.10 = f32[8,16]{1,0:T(8,128)S(1)} collective-permute-done((f32[8,16]{1,0:T(8,128)S(1)}, f32[8,16]{1,0:T(8,128)S(1)}, u32[]{:S(2)}, u32[]{:S(2)}) %collective-permute-start.10) | collective-permute-done | bytes 544 | tf_op jit(solution)/shard_map/ppermute | solution.py:18
  162.4 0.6 fusion.22
  (67 shorter events, 3.1 us)
Async XLA Ops:
  0.0 14.7 %collective-permute-start.7 = (bf16[256,512]{1,0:T(8,128)(2,1)}, bf16[256,512]{1,0:T(8,128)(2,1)S(1)}, u32[]{:S(2)}, u32[]{:S(2)}) collective-permute-start(bf16[256,512]{1,0:T(8,128)(2,1)} %refs_0_.5), channel_id=1, source_target_pairs={{0,32},{16,48},{32,64},{48,80},{64,96},{80,112},{96,128},{112,144}... | collective-permute-start | bytes 786440 | tf_op jit(solution)/shard_map/ppermute | solution.py:18
  3.1 17.5 %collective-permute-start.5 = (bf16[256,512]{1,0:T(8,128)(2,1)}, bf16[256,512]{1,0:T(8,128)(2,1)S(1)}, u32[]{:S(2)}, u32[]{:S(2)}) collective-permute-start(bf16[256,512]{1,0:T(8,128)(2,1)} %refs_0_.5), channel_id=1, source_target_pairs={{16,128},{48,160},{80,192},{112,224},{144,0},{176,32},{208,64},{24... | collective-permute-start | bytes 786440 | tf_op jit(solution)/shard_map/ppermute | solution.py:18
  4.4 16.2 %collective-permute-start.6 = (bf16[256,512]{1,0:T(8,128)(2,1)}, bf16[256,512]{1,0:T(8,128)(2,1)S(1)}, u32[]{:S(2)}, u32[]{:S(2)}) collective-permute-start(bf16[256,512]{1,0:T(8,128)(2,1)} %refs_0_.5), channel_id=1, source_target_pairs={{0,16},{16,0},{32,48},{48,32},{64,80},{80,64},{96,112},{112,96},{1... | collective-permute-start | bytes 786440 | tf_op jit(solution)/shard_map/ppermute | solution.py:18
  7.3 13.4 %collective-permute-start.9 = (bf16[512,256]{1,0:T(8,128)(2,1)}, bf16[512,256]{1,0:T(8,128)(2,1)S(1)}, u32[]{:S(2)}, u32[]{:S(2)}) collective-permute-start(bf16[512,256]{1,0:T(8,128)(2,1)} %refs_4_.3), channel_id=1, source_target_pairs={{0,192},{16,208},{32,224},{48,240},{64,0},{80,16},{96,32},{112,48}... | collective-permute-start | bytes 786440 | tf_op jit(solution)/shard_map/ppermute | solution.py:18
  14.7 6.0 %collective-permute-start.8 = (bf16[256,512]{1,0:T(8,128)(2,1)S(1)}, bf16[256,512]{1,0:T(8,128)(2,1)S(1)}, u32[]{:S(2)}, u32[]{:S(2)}) collective-permute-start(bf16[256,512]{1,0:T(8,128)(2,1)S(1)} %collective-permute-done.7.refs_2_), channel_id=1, source_target_pairs={{0,16},{16,0},{32,48},{48,32},{64,80},{80,64},{96,112},{112,96},{1... | collective-permute-start | bytes 786440 | tf_op jit(solution)/shard_map/ppermute | solution.py:18
  14.7 49.7 %collective-permute-start.2 = (bf16[256,1792]{1,0:T(8,128)(2,1)}, bf16[256,1792]{1,0:T(8,128)(2,1)S(1)}, u32[]{:S(2)}, u32[]{:S(2)}) collective-permute-start(bf16[256,1792]{1,0:T(8,128)(2,1)} %refs_0_.4), channel_id=1, source_target_pairs={{0,32},{16,48},{32,64},{48,80},{64,96},{80,112},{96,128},{112,144}... | collective-permute-start | bytes 2752520 | tf_op jit(solution)/shard_map/ppermute | solution.py:18
  20.6 1.0 copy-start.2
  21.6 0.9 copy-start.3
  25.0 8.9 %copy-start = (bf16[256,1792]{1,0:T(8,128)(2,1)S(1)}, bf16[256,1792]{1,0:T(8,128)(2,1)}, u32[]{:S(2)}) copy-start(bf16[256,1792]{1,0:T(8,128)(2,1)} %refs_0_.4) | copy-start | bytes 2752516
  25.0 39.3 %copy-start.1 = (bf16[1792,256]{1,0:T(8,128)(2,1)S(1)}, bf16[1792,256]{1,0:T(8,128)(2,1)}, u32[]{:S(2)}) copy-start(bf16[1792,256]{1,0:T(8,128)(2,1)} %refs_4_.2) | copy-start | bytes 2752516
  25.0 71.1 %all-to-all-start.1 = ((s16[16,16,2176]{2,1,0:T(8,128)(2,1)}), s16[16,16,2176]{2,1,0:T(8,128)(2,1)}, u32[]{:S(2)}, u32[]{:S(2)}) async-start(s16[16,16,2176]{2,1,0:T(8,128)(2,1)} %bitcast.3), calls=%async_computation.1 | async-start | bytes 2228224 | tf_op jit(solution)/shard_map/all_to_all | solution.py:84
  33.9 30.5 %collective-permute-start = (bf16[256,1792]{1,0:T(8,128)(2,1)S(1)}, bf16[256,1792]{1,0:T(8,128)(2,1)S(1)}, u32[]{:S(2)}, u32[]{:S(2)}) collective-permute-start(bf16[256,1792]{1,0:T(8,128)(2,1)S(1)} %copy-done), channel_id=1, source_target_pairs={{16,128},{48,160},{80,192},{112,224},{144,0},{176,32},{208,64},{24... | collective-permute-start | bytes 2752520 | tf_op jit(solution)/shard_map/ppermute | solution.py:18
  35.2 29.2 %collective-permute-start.1 = (bf16[256,1792]{1,0:T(8,128)(2,1)S(1)}, bf16[256,1792]{1,0:T(8,128)(2,1)S(1)}, u32[]{:S(2)}, u32[]{:S(2)}) collective-permute-start(bf16[256,1792]{1,0:T(8,128)(2,1)S(1)} %copy-done), channel_id=1, source_target_pairs={{0,16},{16,0},{32,48},{48,32},{64,80},{80,64},{96,112},{112,96},{1... | collective-permute-start | bytes 2752520 | tf_op jit(solution)/shard_map/ppermute | solution.py:18
  64.4 2.5 %collective-permute-start.3 = (bf16[256,1792]{1,0:T(8,128)(2,1)S(1)}, bf16[256,1792]{1,0:T(8,128)(2,1)S(1)}, u32[]{:S(2)}, u32[]{:S(2)}) collective-permute-start(bf16[256,1792]{1,0:T(8,128)(2,1)S(1)} %collective-permute-done.2.refs_2_), channel_id=1, source_target_pairs={{0,16},{16,0},{32,48},{48,32},{64,80},{80,64},{96,112},{112,96},{1... | collective-permute-start | bytes 2752520 | tf_op jit(solution)/shard_map/ppermute | solution.py:18
  64.4 29.3 %collective-permute-start.4 = (bf16[1792,256]{1,0:T(8,128)(2,1)S(1)}, bf16[1792,256]{1,0:T(8,128)(2,1)S(1)}, u32[]{:S(2)}, u32[]{:S(2)}) collective-permute-start(bf16[1792,256]{1,0:T(8,128)(2,1)S(1)} %copy-done.1), channel_id=1, source_target_pairs={{0,192},{16,208},{32,224},{48,240},{64,0},{80,16},{96,32},{112,48}... | collective-permute-start | bytes 2752520 | tf_op jit(solution)/shard_map/ppermute | solution.py:18
  96.1 14.5 %copy-start.4 = (s32[256]{0:T(256)S(1)}, s32[256]{0:T(256)}, u32[]{:S(2)}) copy-start(s32[256]{0:T(256)} %param.9) | copy-start | bytes 3076
  96.1 43.5 %all-to-all-start = ((s16[16,16,2304]{2,1,0:T(8,128)(2,1)}), s16[16,16,2304]{2,1,0:T(8,128)(2,1)S(1)}, u32[]{:S(2)}, u32[]{:S(2)}) async-start(s16[16,16,2304]{2,1,0:T(8,128)(2,1)} %bitcast.1), calls=%async_computation | async-start | bytes 2359296 | tf_op jit(solution)/shard_map/all_to_all | solution.py:84
  157.2 5.2 %collective-permute-start.10 = (f32[8,16]{1,0:T(8,128)S(1)}, f32[8,16]{1,0:T(8,128)S(1)}, u32[]{:S(2)}, u32[]{:S(2)}) collective-permute-start(f32[8,16]{1,0:T(8,128)S(1)} %slice.193), channel_id=1, source_target_pairs={{0,64},{16,80},{32,96},{48,112},{64,128},{80,144},{96,160},{112,17... | collective-permute-start | bytes 1544 | tf_op jit(solution)/shard_map/ppermute | solution.py:18

commit v3 on v2

v3 whole, which is shorter than its diff:
```python
import jax
import jax.numpy as jnp
from jax import lax
from jax.experimental import pallas as pl
from jax.experimental.pallas import tpu as pltpu
from jax.sharding import PartitionSpec as P


RANK = 32
LANES = 128
LARGEST = 32000.0
WIDTH = 256


def moved(value, pairs):
    return lax.ppermute(value, "pb", pairs)


def code(part, slot, out_ref):
    width, rows, tags = part.shape[1], out_ref.shape[0], out_ref.shape[1] - LANES
    lane = lax.broadcasted_iota(jnp.int32, (rows, LANES), 1)
    largest = jnp.maximum(jnp.max(jnp.abs(part), axis=1, keepdims=True), 1e-25)
    power = jnp.floor(jnp.log2(LARGEST / largest))
    coded = jnp.round(part * jnp.exp2(power)).astype(jnp.int32)
    out_ref[:, slot * width : (slot + 1) * width] = coded.astype(jnp.int16)
    held = out_ref[:, tags:].astype(jnp.int32)
    tag = jnp.where(lane == slot, power.astype(jnp.int32), held)
    out_ref[:, tags:] = tag.astype(jnp.int16)


def put(slot, tokens, queries, out_ref):
    part = jnp.dot(tokens[...], queries[...], preferred_element_type=jnp.float32)
    code(part, slot, out_ref)


def near_rows(even_ref, own, side, flip, last, lasts, queries, out_ref):
    out_ref[:, out_ref.shape[1] - LANES :] = jnp.zeros((out_ref.shape[0], LANES), jnp.int16)
    put(0, own, queries, out_ref)

    @pl.when(even_ref[0] == 1)
    def _():
        put(1, flip, queries, out_ref)

    @pl.when(even_ref[0] == 0)
    def _():
        put(1, side, queries, out_ref)

    put(2, last, queries, out_ref)
    put(3, lasts, queries, out_ref)


def far_rows(own, side, last, lasts, queries, out_ref):
    put(4, own, queries, out_ref)
    put(5, side, queries, out_ref)
    put(6, last, queries, out_ref)
    put(7, lasts, queries, out_ref)


def rest_kernel(even, own, side, flip, last, lasts, near, far, out_ref):
    near_rows(even, own, side, flip, last, lasts, near, out_ref)
    far_rows(own, side, last, lasts, far, out_ref)


def near_kernel(even, own, side, flip, last, lasts, near, out_ref):
    near_rows(even, own, side, flip, last, lasts, near, out_ref)


def far_kernel(odd_ref, own, side, last, lasts, whole, top, bottom, begun, out_ref, far):
    half, lanes = top.shape[0], begun.shape[1] - LANES

    @pl.when(odd_ref[0] == 1)
    def _():
        far[...] = whole[...]

    @pl.when(odd_ref[0] == 0)
    def _():
        far[:half, :] = top[...]
        far[half:, :] = bottom[...]

    out_ref[:, :lanes] = begun[:, :lanes]
    out_ref[:, out_ref.shape[1] - LANES :] = begun[:, lanes:]
    far_rows(own, side, last, lasts, far, out_ref)


def call(kernel, slots, scalar, arrays, scratch=()):
    rows, depth = arrays[0].shape
    lanes = slots * WIDTH
    vmem = pl.BlockSpec(memory_space=pltpu.VMEM)
    return pl.pallas_call(
        kernel,
        out_shape=jax.ShapeDtypeStruct((rows, lanes + LANES), jnp.int16),
        in_specs=[pl.BlockSpec(memory_space=pltpu.SMEM)] + [vmem] * len(arrays),
        out_specs=vmem,
        scratch_shapes=list(scratch),
        compiler_params=pltpu.CompilerParams(vmem_limit_bytes=16 << 20),
        cost_estimate=pl.CostEstimate(
            flops=2 * rows * depth * lanes,
            bytes_accessed=sum(a.size for a in arrays) * 2 + 2 * rows * lanes,
            transcendentals=0,
        ),
    )(scalar, *arrays)


def summed(coded, widths):
    rows = coded.shape[0] // widths
    came = lax.all_to_all(coded, "wa", 0, 0, tiled=True)
    came = came.reshape(widths, rows, coded.shape[1])
    tags = coded.shape[1] - LANES
    slots = tags // WIDTH
    undo = jnp.exp2(-came[:, :, tags : tags + slots].astype(jnp.float32))
    pieces = []
    for slot in range(slots):
        values = came[:, :, slot * WIDTH : (slot + 1) * WIDTH]
        scale = undo[:, :, slot : slot + 1]
        pieces.append(jnp.sum(values.astype(jnp.float32) * scale, axis=0))
    return pieces


def member_table(starts, ends, first, count):
    spots = first + lax.iota(jnp.int32, count)
    inside = (spots[:, None] >= starts[None, :]) & (spots[:, None] < ends[None, :])
    return inside.astype(jnp.float32)


def scores(acts, grads, query_in, query_out, lengths):
    groups = lax.axis_size("pb")
    widths = lax.axis_size("wa")
    group = lax.axis_index("pb")
    width_slot = lax.axis_index("wa")
    quarter, half = groups // 4, groups // 2
    tok = acts.shape[0]
    rows = tok // widths
    nseq = lengths.shape[0]
    even = group % 2 == 0

    swap = [(p, p ^ 1) for p in range(groups)]
    ahead = [(p, (p + 2) % groups) for p in range(groups)]
    back = [(p, (p - quarter) % groups) for p in range(groups)]
    flip = [(p, (p - 1 + half) % groups) for p in range(1, groups, 2)]

    side_out = moved(grads, swap)
    last_out = moved(grads, ahead)
    far_out = moved(query_out, back)
    flip_out = moved(grads, flip)
    odd_chips = [p for p in range(groups) if p // 2 % 2 == 1]
    even_chips = [p for p in range(groups) if p // 2 % 2 == 0]
    cut = query_in.shape[0] // 2
    top, bottom = query_in[:cut], query_in[cut:]
    hop = moved(bottom, [(p, (p - 2) % groups) for p in even_chips])
    far_whole = moved(query_in, [(p, (p - quarter) % groups) for p in odd_chips])
    side_in = moved(acts, swap)
    last_in = moved(acts, ahead)
    far_top = moved(top, [(p, (p - quarter) % groups) for p in even_chips])
    flip_in = moved(acts, flip)
    far_bottom = moved(hop, [(p, (p - 2) % groups) for p in odd_chips])
    lasts_out = moved(last_out, swap)
    lasts_in = moved(last_in, swap)
    parity = even.astype(jnp.int32).reshape(1)
    odd_chip = (group // 2 % 2).astype(jnp.int32).reshape(1)
    coded_out = call(
        rest_kernel, 8, parity, [grads, side_out, flip_out, last_out, lasts_out, query_out, far_out]
    )
    outs = summed(coded_out, widths)
    near_in = call(near_kernel, 4, parity, [acts, side_in, flip_in, last_in, lasts_in, query_in])
    coded_in = call(
        far_kernel,
        8,
        odd_chip,
        [acts, side_in, last_in, lasts_in, far_whole, far_top, far_bottom, near_in],
        [pltpu.VMEM(query_in.shape, query_in.dtype)],
    )
    ins = summed(coded_in, widths)
    products = [a * b for a, b in zip(ins, outs)]
    ends = jnp.cumsum(lengths)
    starts = ends - lengths

    def table(block):
        return member_table(starts, ends, block * tok + width_slot * rows, rows)

    here, side = group, group ^ 1
    edge = jnp.where(even, (group + groups - half + 1) % groups, side)
    last, lasts = (group + groups - 2) % groups, (side + groups - 2) % groups
    t_own, t_side, t_edge, t_last, t_lasts = [table(b) for b in (here, side, edge, last, lasts)]

    def totals(pieces, tables):
        by_rank = lax.dot_general(
            jnp.concatenate(pieces, axis=0),
            jnp.concatenate(tables, axis=0),
            (((0,), (0,)), ((), ())),
            precision=lax.Precision.HIGHEST,
        )
        return jnp.sum(by_rank.reshape(-1, RANK, nseq), axis=1)

    near_total = totals(products[:4], [t_own, t_edge, t_last, t_lasts])
    far_total = totals(products[4:], [t_own, t_side, t_last, t_lasts])
    share = nseq // widths
    both = jnp.concatenate([near_total, far_total], axis=0)
    both = jnp.moveaxis(both.reshape(both.shape[0], widths, share), 1, 0)
    came = jnp.sum(lax.all_to_all(both, "wa", 0, 0, tiled=True), axis=0)
    queries = near_total.shape[0]
    forward = [(p, (p + quarter) % groups) for p in range(groups)]
    mine = came[:queries] + moved(came[queries:], forward)
    lengths_float = lengths.astype(jnp.float32)
    my_lengths = lax.dynamic_slice_in_dim(lengths_float, width_slot * share, share, 0)
    return mine / my_lengths[None, :]


def solution(mesh):
    return jax.shard_map(
        scores,
        mesh=mesh,
        in_specs=(P("pb", "wa"), P("pb", "wa"), P("wa", "pb"), P("wa", "pb"), P()),
        out_specs=P("pb", "wa"),
        check_vma=False,
    )
```

time: 163 us -> 171 us (1.049); the launches traced: 163 us -> 168 us
  Pallas kernels: 5.62 us -> 10.1 us
  local copies, waits for them, and re-layouts: 5.98 us -> 7.75 us
    pallas_call x3, Pallas kernels: 5.62 us -> 10.1 us  [call(): pl.pallas_call(kernel, out_shape=jax.ShapeDtypeStruct((rows, lanes + LANE...]
    all_to_all x2, starting transfers between devices: 23.3 us -> 19.7 us  [summed(): came = lax.all_to_all(coded, 'wa', 0, 0, tiled=True)]
    ppermute x11 -> x14, starting transfers between devices: 17.6 us -> 20.1 us  [moved(): return lax.ppermute(value, 'pb', pairs)]
    slice x3 -> x4, local copies, waits for them, and re-layouts: 0.94 us -> 2.96 us  [the longest x1 2.02 us: scores(): top, bottom = (query_in[:cut], query_in[cut:])]
    ppermute x11 -> x14, waiting for transfers between devices: 66.1 us -> 67.8 us  [moved(): return lax.ppermute(value, 'pb', pairs)]
    unnamed x31 -> x28, local copies, waits for them, and re-layouts: 4.18 us -> 3.93 us
  transfers between devices with their start and end apart: 13 -> 16, of which waited for: 6 -> 6; matrix products, arithmetic and copies ran while one was open for 3% -> 4% of each run, Pallas kernels for 3% -> 6%
where the time goes in v3:
time: 171 us; the launch traced here: 168 us
  waiting for transfers between devices  91.5 us (54%)
  starting transfers between devices  39.8 us (23%)
  blocking collectives  12.8 us (7%)
  Pallas kernels  10.1 us (6%)
  local copies, waits for them, and re-layouts  7.75 us (5%)
  other arithmetic  4.21 us (2%)
    ppermute x14, waiting for transfers between devices, moved(): return lax.ppermute(value, 'pb', pairs)  67.8 us
    all_to_all x2, waiting for transfers between devices, summed(): came = lax.all_to_all(coded, 'wa', 0, 0, tiled=True)  23.6 us
    ppermute x14, starting transfers between devices, moved(): return lax.ppermute(value, 'pb', pairs)  20.1 us
    all_to_all x2, starting transfers between devices, summed(): came = lax.all_to_all(coded, 'wa', 0, 0, tiled=True)  19.7 us
    all_to_all x1, blocking collectives, scores(): came = jnp.sum(lax.all_to_all(both, 'wa', 0, 0, tiled=True), axis=0)  12.8 us
    pallas_call x3, Pallas kernels, call(): pl.pallas_call(kernel, out_shape=jax.ShapeDtypeStruct((rows, lanes + LANE...  10.1 us
    unnamed x28, local copies, waits for them, and re-layouts  3.93 us
  transfers between devices with their start and end apart: 16, of which 6 were waited for; matrix products, arithmetic and copies ran while one was open for 4% of the time, Pallas kernels for 6%

profile of v3, /device:TPU:6, one launch (start us, length us, event | category | flops | bytes accessed | tf_op | source)
XLA Modules:
  0.0 167.6 jit_solution(3402826876745926997)
XLA Ops:
  0.0 3.1 %collective-permute-start.10 = (bf16[256,512]{1,0:T(8,128)(2,1)}, bf16[256,512]{1,0:T(8,128)(2,1)S(1)}, u32[]{:S(2)}, u32[]{:S(2)}) collective-permute-start(bf16[256,512]{1,0:T(8,128)(2,1)} %own.5), channel_id=1, source_target_pairs={{0,32},{16,48},{32,64},{48,80},{64,96},{80,112},{96,128},{112,144}... | collective-permute-start | bytes 786440 | tf_op jit(solution)/shard_map/ppermute | solution.py:16
  3.1 1.3 collective-permute-start.9
  4.5 10.1 %collective-permute-done.10.last = bf16[256,512]{1,0:T(8,128)(2,1)S(1)} collective-permute-done((bf16[256,512]{1,0:T(8,128)(2,1)}, bf16[256,512]{1,0:T(8,128)(2,1)S(1)}, u32[]{:S(2)}, u32[]{:S(2)}) %collective-permute-start.10) | collective-permute-done | bytes 262176 | tf_op jit(solution)/shard_map/ppermute | solution.py:16
  14.6 6.0 %collective-permute-start.1 = (bf16[256,1792]{1,0:T(8,128)(2,1)}, bf16[256,1792]{1,0:T(8,128)(2,1)S(1)}, u32[]{:S(2)}, u32[]{:S(2)}) collective-permute-start(bf16[256,1792]{1,0:T(8,128)(2,1)} %own.4), channel_id=1, source_target_pairs={{0,32},{16,48},{32,64},{48,80},{64,96},{80,112},{96,128},{112,144}... | collective-permute-start | bytes 2752520 | tf_op jit(solution)/shard_map/ppermute | solution.py:16
  20.6 0.9 copy-done.1
  21.6 0.9 copy-done.2
  22.5 2.5 %shard_map.57 = s16[256,2176]{1,0:T(8,128)(2,1)} custom-call(s32[1]{0:T(128)} %bitcast.1.even, bf16[256,512]{1,0:T(8,128)(2,1)S(1)} %copy-done.1, bf16[256,512]{1,0:T(8,128)(2,1)S(1)} %collective-permute-done.8.side, bf16[256,512]{1,0:T(8,128)(2,1)S(1)} %collective-permute-done.9.flip, bf16[256,512]{1,0:T(8,128)(2,1)S(1)} %collective-permute-done.10.last, ...), custom_call_target="tpu_custom_call" | custom-call | flops 536870912 | bytes 2883584 | tf_op jit(solution)/shard_map/pallas_call | solution.py:89
  25.1 8.9 %all-to-all-start.1 = ((s16[16,16,2176]{2,1,0:T(8,128)(2,1)}), s16[16,16,2176]{2,1,0:T(8,128)(2,1)}, u32[]{:S(2)}, u32[]{:S(2)}) async-start(s16[16,16,2176]{2,1,0:T(8,128)(2,1)} %bitcast.4), calls=%async_computation.1 | async-start | bytes 2228224 | tf_op jit(solution)/shard_map/all_to_all | solution.py:106
  34.1 1.3 collective-permute-start.7
  35.4 11.6 %collective-permute-done.1.last = bf16[256,1792]{1,0:T(8,128)(2,1)S(1)} collective-permute-done((bf16[256,1792]{1,0:T(8,128)(2,1)}, bf16[256,1792]{1,0:T(8,128)(2,1)S(1)}, u32[]{:S(2)}, u32[]{:S(2)}) %collective-permute-start.1) | collective-permute-done | bytes 917536 | tf_op jit(solution)/shard_map/ppermute | solution.py:16
  47.0 2.0 %fusion.26 = (bf16[896,256]{1,0:T(8,128)(2,1)S(1)}, bf16[896,256]{1,0:T(8,128)(2,1)}) fusion(bf16[1792,256]{1,0:T(8,128)(2,1)} %near.2), kind=kLoop, calls=%fused_computation.78 | loop fusion | bytes 1835008 | tf_op jit(solution)/shard_map/slice | solution.py:148
  49.0 1.3 collective-permute-start.5
  50.3 1.9 %collective-permute-start.3 = (bf16[1792,256]{1,0:T(8,128)(2,1)}, bf16[1792,256]{1,0:T(8,128)(2,1)}, u32[]{:S(2)}, u32[]{:S(2)}) collective-permute-start(bf16[1792,256]{1,0:T(8,128)(2,1)} %near.2), channel_id=1, source_target_pairs={{32,224},{48,240},{96,32},{112,48},{160,96},{176,112},{224,160},{2... | collective-permute-start | bytes 2752520 | tf_op jit(solution)/shard_map/ppermute | solution.py:16
  52.2 37.0 %collective-permute-done.5 = bf16[896,256]{1,0:T(8,128)(2,1)} collective-permute-done((bf16[896,256]{1,0:T(8,128)(2,1)S(1)}, bf16[896,256]{1,0:T(8,128)(2,1)}, u32[]{:S(2)}, u32[]{:S(2)}) %collective-permute-start.5) | collective-permute-done | bytes 458784 | tf_op jit(solution)/shard_map/ppermute | solution.py:16
  89.2 0.7 collective-permute-start.4
  89.9 2.1 %collective-permute-start.6 = (bf16[896,256]{1,0:T(8,128)(2,1)}, bf16[896,256]{1,0:T(8,128)(2,1)}, u32[]{:S(2)}, u32[]{:S(2)}) collective-permute-start(bf16[896,256]{1,0:T(8,128)(2,1)} %collective-permute-done.5), channel_id=1, source_target_pairs={{32,0},{48,16},{96,64},{112,80},{160,128},{176,144},{224,192},{240... | collective-permute-start | bytes 1376264 | tf_op jit(solution)/shard_map/ppermute | solution.py:16
  92.0 3.6 %shard_map.55.begun = s16[256,1152]{1,0:T(8,128)(2,1)S(1)} custom-call(s32[1]{0:T(128)} %bitcast.1.even, bf16[256,1792]{1,0:T(8,128)(2,1)S(1)} %copy-done, bf16[256,1792]{1,0:T(8,128)(2,1)S(1)} %collective-permute-done.side, bf16[256,1792]{1,0:T(8,128)(2,1)} %collective-permute-done.7.flip, bf16[256,1792]{1,0:T(8,128)(2,1)S(1)} %collective-permute-done.1.last, ...), custom_call_target="tpu_custom_call" | custom-call | flops 939524096 | bytes 6029312 | tf_op jit(solution)/shard_map/pallas_call | solution.py:89
  95.6 6.2 %collective-permute-done.6.bottom = bf16[896,256]{1,0:T(8,128)(2,1)} collective-permute-done((bf16[896,256]{1,0:T(8,128)(2,1)}, bf16[896,256]{1,0:T(8,128)(2,1)}, u32[]{:S(2)}, u32[]{:S(2)}) %collective-permute-start.6) | collective-permute-done | bytes 458784 | tf_op jit(solution)/shard_map/ppermute | solution.py:16
  101.8 4.0 %shard_map.56 = s16[256,2176]{1,0:T(8,128)(2,1)} custom-call(s32[1]{0:T(128)} %bitcast.odd_ref, bf16[256,1792]{1,0:T(8,128)(2,1)S(1)} %copy-done, bf16[256,1792]{1,0:T(8,128)(2,1)S(1)} %collective-permute-done.side, bf16[256,1792]{1,0:T(8,128)(2,1)S(1)} %collective-permute-done.1.last, bf16[256,1792]{1,0:T(8,128)(2,1)} %collective-permute-done.2.lasts, ...), custom_call_target="tpu_custom_call" | custom-call | flops 1879048192 | bytes 7143424 | tf_op jit(solution)/shard_map/pallas_call | solution.py:89
  105.8 10.9 %all-to-all-start = ((s16[16,16,2176]{2,1,0:T(8,128)(2,1)}), s16[16,16,2176]{2,1,0:T(8,128)(2,1)S(1)}, u32[]{:S(2)}, u32[]{:S(2)}) async-start(s16[16,16,2176]{2,1,0:T(8,128)(2,1)} %bitcast.2), calls=%async_computation | async-start | bytes 2228224 | tf_op jit(solution)/shard_map/all_to_all | solution.py:106
  117.5 0.8 slice.165
  118.5 1.8 %multiply_reduce_fusion.14 = (f32[16,256]{1,0:T(8,128)S(1)}, f32[16,256]{1,0:T(8,128)S(1)}, f32[16,256]{1,0:T(8,128)S(1)}, f32[16,256]{1,0:T(8,128)S(1)}, f32[16...) fusion(s16[16,16,2176]{2,1,0:T(8,128)(2,1)} %all-to-all-done.1, ...), kind=kLoop, calls=%fused_computation.16 | loop fusion | flops 1540096 | bytes 1187840 | tf_op jit(solution)/shard_map/reduce_sum | solution.py:115
  121.0 23.6 %all-to-all-done = s16[16,16,2176]{2,1,0:T(8,128)(2,1)S(1)} async-done(((s16[16,16,2176]{2,1,0:T(8,128)(2,1)}), s16[16,16,2176]{2,1,0:T(8,128)(2,1)S(1)}, u32[]{:S(2)}, u32[]{:S(2)}) %all-to-all-start) | async-done | bytes 1114144 | tf_op jit(solution)/shard_map/all_to_all | solution.py:106
  144.9 0.4 multiply_reduce_fusion.15
  146.3 0.5 bitcast_reduce_fusion
  146.9 0.5 bitcast_reduce_fusion.1
  147.7 12.8 %all_to_all.23 = f32[16,1,256]{2,1,0:T(1,128)S(1)} all-to-all(f32[16,1,256]{2,1,0:T(1,128)S(1)} %reshape.84), channel_id=1, replica_groups=mesh['pb'=16,'wa'=16] {'wa'}, dimensions={0} | all-to-all | bytes 32768 | tf_op jit(solution)/shard_map/all_to_all | solution.py:199
  160.5 0.5 broadcast.44
  161.0 0.7 reduce.2
  161.8 2.3 %collective-permute-start.13 = (f32[8,16]{1,0:T(8,128)S(1)}, f32[8,16]{1,0:T(8,128)S(1)}, u32[]{:S(2)}, u32[]{:S(2)}) collective-permute-start(f32[8,16]{1,0:T(8,128)S(1)} %slice.196), channel_id=1, source_target_pairs={{0,64},{16,80},{32,96},{48,112},{64,128},{80,144},{96,160},{112,17... | collective-permute-start | bytes 1544 | tf_op jit(solution)/shard_map/ppermute | solution.py:16
  164.2 2.9 %collective-permute-done.13 = f32[8,16]{1,0:T(8,128)S(1)} collective-permute-done((f32[8,16]{1,0:T(8,128)S(1)}, f32[8,16]{1,0:T(8,128)S(1)}, u32[]{:S(2)}, u32[]{:S(2)}) %collective-permute-start.13) | collective-permute-done | bytes 544 | tf_op jit(solution)/shard_map/ppermute | solution.py:16
  167.0 0.6 fusion.22
  (69 shorter events, 3.4 us)
Async XLA Ops:
  0.0 14.6 %collective-permute-start.10 = (bf16[256,512]{1,0:T(8,128)(2,1)}, bf16[256,512]{1,0:T(8,128)(2,1)S(1)}, u32[]{:S(2)}, u32[]{:S(2)}) collective-permute-start(bf16[256,512]{1,0:T(8,128)(2,1)} %own.5), channel_id=1, source_target_pairs={{0,32},{16,48},{32,64},{48,80},{64,96},{80,112},{96,128},{112,144}... | collective-permute-start | bytes 786440 | tf_op jit(solution)/shard_map/ppermute | solution.py:16
  3.1 17.5 %collective-permute-start.8 = (bf16[256,512]{1,0:T(8,128)(2,1)}, bf16[256,512]{1,0:T(8,128)(2,1)S(1)}, u32[]{:S(2)}, u32[]{:S(2)}) collective-permute-start(bf16[256,512]{1,0:T(8,128)(2,1)} %own.5), channel_id=1, source_target_pairs={{0,16},{16,0},{32,48},{48,32},{64,80},{80,64},{96,112},{112,96},{1... | collective-permute-start | bytes 786440 | tf_op jit(solution)/shard_map/ppermute | solution.py:16
  3.1 17.5 %collective-permute-start.9 = (bf16[256,512]{1,0:T(8,128)(2,1)}, bf16[256,512]{1,0:T(8,128)(2,1)S(1)}, u32[]{:S(2)}, u32[]{:S(2)}) collective-permute-start(bf16[256,512]{1,0:T(8,128)(2,1)} %own.5), channel_id=1, source_target_pairs={{16,128},{48,160},{80,192},{112,224},{144,0},{176,32},{208,64},{24... | collective-permute-start | bytes 786440 | tf_op jit(solution)/shard_map/ppermute | solution.py:16
  4.4 16.2 %collective-permute-start.12 = (bf16[512,256]{1,0:T(8,128)(2,1)}, bf16[512,256]{1,0:T(8,128)(2,1)S(1)}, u32[]{:S(2)}, u32[]{:S(2)}) collective-permute-start(bf16[512,256]{1,0:T(8,128)(2,1)} %near.3), channel_id=1, source_target_pairs={{0,192},{16,208},{32,224},{48,240},{64,0},{80,16},{96,32},{112,48}... | collective-permute-start | bytes 786440 | tf_op jit(solution)/shard_map/ppermute | solution.py:16
  14.6 6.0 %collective-permute-start.11 = (bf16[256,512]{1,0:T(8,128)(2,1)S(1)}, bf16[256,512]{1,0:T(8,128)(2,1)S(1)}, u32[]{:S(2)}, u32[]{:S(2)}) collective-permute-start(bf16[256,512]{1,0:T(8,128)(2,1)S(1)} %collective-permute-done.10.last), channel_id=1, source_target_pairs={{0,16},{16,0},{32,48},{48,32},{64,80},{80,64},{96,112},{112,96},{1... | collective-permute-start | bytes 786440 | tf_op jit(solution)/shard_map/ppermute | solution.py:16
  14.6 32.4 %collective-permute-start.1 = (bf16[256,1792]{1,0:T(8,128)(2,1)}, bf16[256,1792]{1,0:T(8,128)(2,1)S(1)}, u32[]{:S(2)}, u32[]{:S(2)}) collective-permute-start(bf16[256,1792]{1,0:T(8,128)(2,1)} %own.4), channel_id=1, source_target_pairs={{0,32},{16,48},{32,64},{48,80},{64,96},{80,112},{96,128},{112,144}... | collective-permute-start | bytes 2752520 | tf_op jit(solution)/shard_map/ppermute | solution.py:16
  20.6 1.0 copy-start.1
  21.6 0.9 copy-start.2
  25.1 8.9 %copy-start = (bf16[256,1792]{1,0:T(8,128)(2,1)S(1)}, bf16[256,1792]{1,0:T(8,128)(2,1)}, u32[]{:S(2)}) copy-start(bf16[256,1792]{1,0:T(8,128)(2,1)} %own.4) | copy-start | bytes 2752516
  25.1 80.7 %all-to-all-start.1 = ((s16[16,16,2176]{2,1,0:T(8,128)(2,1)}), s16[16,16,2176]{2,1,0:T(8,128)(2,1)}, u32[]{:S(2)}, u32[]{:S(2)}) async-start(s16[16,16,2176]{2,1,0:T(8,128)(2,1)} %bitcast.4), calls=%async_computation.1 | async-start | bytes 2228224 | tf_op jit(solution)/shard_map/all_to_all | solution.py:106
  34.0 56.0 %collective-permute-start = (bf16[256,1792]{1,0:T(8,128)(2,1)S(1)}, bf16[256,1792]{1,0:T(8,128)(2,1)S(1)}, u32[]{:S(2)}, u32[]{:S(2)}) collective-permute-start(bf16[256,1792]{1,0:T(8,128)(2,1)S(1)} %copy-done), channel_id=1, source_target_pairs={{0,16},{16,0},{32,48},{48,32},{64,80},{80,64},{96,112},{112,96},{1... | collective-permute-start | bytes 2752520 | tf_op jit(solution)/shard_map/ppermute | solution.py:16
  34.1 58.0 %collective-permute-start.7 = (bf16[256,1792]{1,0:T(8,128)(2,1)S(1)}, bf16[256,1792]{1,0:T(8,128)(2,1)}, u32[]{:S(2)}, u32[]{:S(2)}) collective-permute-start(bf16[256,1792]{1,0:T(8,128)(2,1)S(1)} %copy-done), channel_id=1, source_target_pairs={{16,128},{48,160},{80,192},{112,224},{144,0},{176,32},{208,64},{24... | collective-permute-start | bytes 2752520 | tf_op jit(solution)/shard_map/ppermute | solution.py:16
  47.0 45.0 %collective-permute-start.2 = (bf16[256,1792]{1,0:T(8,128)(2,1)S(1)}, bf16[256,1792]{1,0:T(8,128)(2,1)}, u32[]{:S(2)}, u32[]{:S(2)}) collective-permute-start(bf16[256,1792]{1,0:T(8,128)(2,1)S(1)} %collective-permute-done.1.last), channel_id=1, source_target_pairs={{0,16},{16,0},{32,48},{48,32},{64,80},{80,64},{96,112},{112,96},{1... | collective-permute-start | bytes 2752520 | tf_op jit(solution)/shard_map/ppermute | solution.py:16
  49.0 40.2 %collective-permute-start.5 = (bf16[896,256]{1,0:T(8,128)(2,1)S(1)}, bf16[896,256]{1,0:T(8,128)(2,1)}, u32[]{:S(2)}, u32[]{:S(2)}) collective-permute-start(bf16[896,256]{1,0:T(8,128)(2,1)S(1)} %get-tuple-element.23), channel_id=1, source_target_pairs={{0,224},{16,240},{64,32},{80,48},{128,96},{144,112},{192,160},{208... | collective-permute-start | bytes 1376264 | tf_op jit(solution)/shard_map/ppermute | solution.py:16
  50.3 45.3 %collective-permute-start.3 = (bf16[1792,256]{1,0:T(8,128)(2,1)}, bf16[1792,256]{1,0:T(8,128)(2,1)}, u32[]{:S(2)}, u32[]{:S(2)}) collective-permute-start(bf16[1792,256]{1,0:T(8,128)(2,1)} %near.2), channel_id=1, source_target_pairs={{32,224},{48,240},{96,32},{112,48},{160,96},{176,112},{224,160},{2... | collective-permute-start | bytes 2752520 | tf_op jit(solution)/shard_map/ppermute | solution.py:16
  89.2 6.4 %collective-permute-start.4 = (bf16[896,256]{1,0:T(8,128)(2,1)}, bf16[896,256]{1,0:T(8,128)(2,1)S(1)}, u32[]{:S(2)}, u32[]{:S(2)}) collective-permute-start(bf16[896,256]{1,0:T(8,128)(2,1)} %get-tuple-element.24), channel_id=1, source_target_pairs={{0,192},{16,208},{64,0},{80,16},{128,64},{144,80},{192,128},{208,1... | collective-permute-start | bytes 1376264 | tf_op jit(solution)/shard_map/ppermute | solution.py:16
  89.9 11.9 %collective-permute-start.6 = (bf16[896,256]{1,0:T(8,128)(2,1)}, bf16[896,256]{1,0:T(8,128)(2,1)}, u32[]{:S(2)}, u32[]{:S(2)}) collective-permute-start(bf16[896,256]{1,0:T(8,128)(2,1)} %collective-permute-done.5), channel_id=1, source_target_pairs={{32,0},{48,16},{96,64},{112,80},{160,128},{176,144},{224,192},{240... | collective-permute-start | bytes 1376264 | tf_op jit(solution)/shard_map/ppermute | solution.py:16
  105.8 10.9 %copy-start.3 = (s32[256]{0:T(256)S(1)}, s32[256]{0:T(256)}, u32[]{:S(2)}) copy-start(s32[256]{0:T(256)} %param.9) | copy-start | bytes 3076
  105.8 38.9 %all-to-all-start = ((s16[16,16,2176]{2,1,0:T(8,128)(2,1)}), s16[16,16,2176]{2,1,0:T(8,128)(2,1)S(1)}, u32[]{:S(2)}, u32[]{:S(2)}) async-start(s16[16,16,2176]{2,1,0:T(8,128)(2,1)} %bitcast.2), calls=%async_computation | async-start | bytes 2228224 | tf_op jit(solution)/shard_map/all_to_all | solution.py:106
  161.8 5.2 %collective-permute-start.13 = (f32[8,16]{1,0:T(8,128)S(1)}, f32[8,16]{1,0:T(8,128)S(1)}, u32[]{:S(2)}, u32[]{:S(2)}) collective-permute-start(f32[8,16]{1,0:T(8,128)S(1)} %slice.196), channel_id=1, source_target_pairs={{0,64},{16,80},{32,96},{48,112},{64,128},{80,144},{96,160},{112,17... | collective-permute-start | bytes 1544 | tf_op jit(solution)/shard_map/ppermute | solution.py:16
